TPU v7x, 32 devices: a whole 2x2x4 slice. The times are simulated.
32 devices in a mesh: rep: 8 (over y, x, core), tp: 4 (over z).
Axes of the slice: x: 2, y: 2, z: 4, core: 2. Of those that a mesh axis runs over, the one named last changes fastest.
Arguments:
- hidden: bfloat16 [512, 8192], P('rep'), may hold values from -6 to 6
- norm_gain: bfloat16 [8192], replicated, may hold values from 0.5 to 1.5
- query_weight_matrix: bfloat16 [8192, 4096], P(None, 'tp'), may hold values from -0.0625 to 0.0625
- key_value_weight: bfloat16 [2, 8192, 1024], P(None, None, 'tp'), may hold values from -0.0625 to 0.0625
- output_weight_matrix: bfloat16 [4096, 8192], P('tp'), may hold values from -0.375 to 0.375
- input_down_factors: bfloat16 [3, 8192, 64], P(None, ('rep', 'tp')), may hold values from -0.0625 to 0.0625
- query_up_factor: bfloat16 [64, 4096], P(None, ('rep', 'tp')), may hold values from -0.75 to 0.75
- key_value_up_factors: bfloat16 [2, 64, 1024], P(None, None, ('rep', 'tp')), may hold values from -0.75 to 0.75
- output_down_factor: bfloat16 [4096, 64], P(('rep', 'tp')), may hold values from -0.375 to 0.375
- output_up_factor: bfloat16 [64, 8192], P(None, ('rep', 'tp')), may hold values from -0.75 to 0.75
- cache_keys: bfloat16 [512, 8, 128, 128], P('rep', 'tp'), may hold values from -360 to 360
- cache_values: bfloat16 [512, 8, 128, 128], P('rep', 'tp'), may hold values from -6 to 6
- lengths: int32 [512], P('rep'), may hold values from 1 to 127
Outputs:
- attn_out: bfloat16 [512, 8192], P('rep', 'tp')
All inputs are finite; a program needn't handle non-finite values.
Results may differ from a plain program's by a relative error of at most 0.03.
Values may be sent and summed in bfloat16 or wider, within the bound.
No kernel may reach another device: no remote copies, remote signals or barrier semaphores. Data moves between devices by JAX's collectives and lax.ppermute only.
A program may use at most 128 MiB of HBM per device.

v0:
```python
import functools
import math

import jax
import jax.numpy as jnp
from jax import lax
from jax.experimental import pallas as pl
from jax.experimental.pallas import tpu as pltpu
from jax.sharding import PartitionSpec as P


epsilon = 1e-06
rope_base = 1000000.0
adapter_scale = 0.5
F32 = jnp.float32
BF16 = jnp.bfloat16


def params(mib=24):
    return pltpu.CompilerParams(vmem_limit_bytes=mib * 1024 * 1024)


def whole(shape):
    return pl.BlockSpec(shape, lambda *_: (0,) * len(shape))


def power_of_two(n):
    return n & (n - 1) == 0


def exchange(n):
    if power_of_two(n):
        return lambda i, k: i ^ k
    return lambda i, k: (i + k) % n


def hop(x, axis, k):
    n = lax.axis_size(axis)
    to = exchange(n)
    return lax.ppermute(x, axis, [(i, to(i, k)) for i in range(n)])


def came_from(index, n, k):
    if power_of_two(n):
        return index ^ k
    return (index - k) % n


def gather_rep(block):
    n = lax.axis_size("rep")
    r = lax.axis_index("rep")
    if not power_of_two(n) or n == 1:
        return [block] + [hop(block, "rep", k) for k in range(1, n)], [
            came_from(r, n, k) for k in range(n)
        ]
    near = [block] + [hop(block, "rep", k) for k in range(2, n, 2)]
    order = [r ^ k for k in range(0, n, 2)]
    return near + [hop(b, "rep", 1) for b in near], order + [o ^ 1 for o in order]


def pack_kernel(q_ref, od_ref, ou_ref, kv_ref, out_ref):
    both = jnp.concatenate([kv_ref[0], kv_ref[1]], axis=0).astype(F32).T.astype(BF16)
    lane = 0
    for piece in (q_ref[...], od_ref[...], ou_ref[...], both):
        out_ref[:, lane : lane + piece.shape[1]] = piece
        lane += piece.shape[1]


def pack(q_up, od, ou, kv_up):
    widths = (q_up.shape[1], od.shape[0], ou.shape[1], kv_up.shape[2], kv_up.shape[2])
    if any(w % 128 for w in widths[:3]):
        return jnp.concatenate([q_up, od.T, ou, kv_up[0], kv_up[1]], axis=1), widths
    vmem = pl.BlockSpec(memory_space=pltpu.VMEM)
    packed = pl.pallas_call(
        pack_kernel,
        in_specs=[vmem] * 4,
        out_specs=vmem,
        out_shape=jax.ShapeDtypeStruct((q_up.shape[0], sum(widths)), BF16),
        compiler_params=params(60),
        name="pack",
    )(q_up, od.T, ou, kv_up.transpose(0, 2, 1))
    return packed, widths


def base_kernel(
    lengths_ref, gain_ref, hidden_hbm, q_hbm, kv_hbm, x_ref, cos_ref, sin_ref, q_out, kv_out,
    hidden, q_held, kv_held, angle, first_sem, q_sems, kv_sems,
):
    count, depth = q_held.shape[0], q_held.shape[1]
    rows, wide = hidden.shape

    def q_copy(i):
        return pltpu.make_async_copy(
            q_hbm.at[pl.ds(i * depth, depth), :], q_held.at[i], q_sems.at[i]
        )

    def kv_copy(i):
        return pltpu.make_async_copy(
            kv_hbm.at[:, pl.ds(i * depth, depth), :], kv_held.at[i], kv_sems.at[i]
        )

    first = pltpu.make_async_copy(hidden_hbm, hidden, first_sem)
    lead = min(4, count)
    first.start()
    for i in range(lead):
        q_copy(i).start()
        kv_copy(i).start()

    dim = cos_ref.shape[1]
    spot = lax.broadcasted_iota(jnp.int32, (1, dim), 1) % (dim // 2)
    freq = jnp.ones((1, dim), F32)
    for bit in range((dim // 2 - 1).bit_length()):
        power = rope_base ** (-(2.0 ** (bit + 1)) / dim)
        freq *= jnp.where((spot >> bit) % 2 == 1, power, 1.0)
    for s in range(rows):
        angle[s : s + 1, :] = freq * lengths_ref[s].astype(F32)
    low = lax.broadcasted_iota(jnp.int32, (rows, dim), 1) < dim // 2
    wave = jnp.sin(angle[...] + jnp.where(low, 0.0, math.pi / 2))
    other = pltpu.roll(wave, dim // 2, 1)
    cos_ref[...] = jnp.where(low, other, wave)
    sin_ref[...] = jnp.where(low, -wave, other)
    q_out[...] = jnp.zeros_like(q_out)
    kv_out[...] = jnp.zeros_like(kv_out)

    first.wait()
    part = gain_ref.shape[1]
    square = jnp.zeros((rows, part), F32)
    for j in range(wide // part):
        states = hidden[:, j * part : (j + 1) * part].astype(F32)
        square += states * states
    factor = lax.rsqrt(jnp.sum(square, axis=-1, keepdims=True) / wide + epsilon)
    for j in range(wide // part):
        lane = slice(j * part, (j + 1) * part)
        scaled = hidden[:, lane].astype(F32) * factor * gain_ref[j : j + 1, :].astype(F32)
        x_ref[:, lane] = scaled.astype(BF16)

    def step(i):
        x = x_ref[:, pl.ds(pl.multiple_of(i * depth, depth), depth)]
        q_copy(i).wait()
        q_out[...] += jnp.dot(x, q_held[i], preferred_element_type=F32)
        kv_copy(i).wait()
        for j in range(kv_hbm.shape[0]):
            kv_out[j] += jnp.dot(x, kv_held[i, j], preferred_element_type=F32)
        return 0

    def fed(i, _):
        @pl.when(i + lead < count)
        def _():
            q_copy(i + lead).start()
            kv_copy(i + lead).start()

        return step(i)

    lax.fori_loop(0, count, fed, 0)


def base_projections(hidden, gain, lengths, q_weights, kv_weights, dim):
    rows, wide = hidden.shape
    depth = 512
    count = wide // depth
    q_cols, kv_cols = q_weights.shape[1], kv_weights.shape[2]
    pair = kv_weights.shape[0]
    vmem = pl.BlockSpec(memory_space=pltpu.VMEM)
    hbm = pl.BlockSpec(memory_space=pltpu.HBM)
    return pl.pallas_call(
        base_kernel,
        in_specs=[pl.BlockSpec(memory_space=pltpu.SMEM), vmem, hbm, hbm, hbm],
        out_specs=[vmem] * 5,
        out_shape=[
            jax.ShapeDtypeStruct((rows, wide), BF16),
            jax.ShapeDtypeStruct((rows, dim), F32),
            jax.ShapeDtypeStruct((rows, dim), F32),
            jax.ShapeDtypeStruct((rows, q_cols), F32),
            jax.ShapeDtypeStruct((pair, rows, kv_cols), F32),
        ],
        scratch_shapes=[
            pltpu.VMEM((rows, wide), BF16),
            pltpu.VMEM((count, depth, q_cols), BF16),
            pltpu.VMEM((count, pair, depth, kv_cols), BF16),
            pltpu.VMEM((rows, dim), F32),
            pltpu.SemaphoreType.DMA(()),
            pltpu.SemaphoreType.DMA((count,)),
            pltpu.SemaphoreType.DMA((count,)),
        ],
        compiler_params=params(52),
        cost_estimate=pl.CostEstimate(
            flops=16 * rows * (q_weights.size + kv_weights.size),
            bytes_accessed=2 * (q_weights.size + kv_weights.size),
            transcendentals=0,
        ),
        name="base",
    )(lengths, gain.reshape(wide // 128, 128), hidden, q_weights, kv_weights)


def inner_kernel(starts_ref, x_ref, *refs):
    blocks, out_ref = refs[:-1], refs[-1]
    ranks, deep = blocks[0].shape
    total = jnp.zeros((x_ref.shape[0], ranks), F32)
    for j, block in enumerate(blocks):
        at = pl.multiple_of(starts_ref[j] * deep, deep)
        total += lax.dot_general(
            x_ref[:, pl.ds(at, deep)],
            block[...],
            (((1,), (1,)), ((), ())),
            preferred_element_type=F32,
        )
    rest = jnp.zeros((x_ref.shape[0], out_ref.shape[1] - ranks), F32)
    out_ref[...] = jnp.concatenate([total, rest], axis=1).astype(BF16)


def partial_inner(normed, blocks, places):
    ranks, deep = blocks[0].shape
    rows = normed.shape[0]
    padded = -(-ranks // 128) * 128
    if deep % 128 == 0:
        return pl.pallas_call(
            inner_kernel,
            grid_spec=pltpu.PrefetchScalarGridSpec(
                num_scalar_prefetch=1,
                grid=(1,),
                in_specs=[whole(normed.shape)] + [whole(b.shape) for b in blocks],
                out_specs=whole((rows, padded)),
            ),
            out_shape=jax.ShapeDtypeStruct((rows, padded), BF16),
            compiler_params=params(8),
            cost_estimate=pl.CostEstimate(
                flops=2 * rows * deep * ranks * len(blocks),
                bytes_accessed=2 * deep * ranks * len(blocks),
                transcendentals=0,
            ),
            name="inner",
        )(jnp.stack(places).astype(jnp.int32), normed, *blocks)
    total = jnp.zeros((rows, ranks), F32)
    for place, block in zip(places, blocks):
        own = lax.dynamic_slice_in_dim(normed, place * deep, deep, 1)
        total += jnp.dot(own, block.T, preferred_element_type=F32)
    return jnp.pad(total, ((0, 0), (0, padded - ranks))).astype(BF16)


def assemble_kernel(order_ref, *refs, widths, count):
    blocks, outs = refs[:count], refs[count:]
    offset = 0
    for width, out_ref in zip(widths, outs):
        total = out_ref.shape[1]
        if width % 128 == 0:
            for j, block in enumerate(blocks):
                at = pl.multiple_of(order_ref[j] * width, 128)
                out_ref[:, pl.ds(at, width)] = block[:, offset : offset + width]
        else:
            placed = jnp.zeros((out_ref.shape[0], total), F32)
            source = lax.broadcasted_iota(jnp.int32, (width, total), 0)
            target = lax.broadcasted_iota(jnp.int32, (width, total), 1)
            for j, block in enumerate(blocks):
                chosen = (target == source + order_ref[j] * width).astype(BF16)
                placed += jnp.dot(
                    block[:, offset : offset + width], chosen, preferred_element_type=F32
                )
            out_ref[...] = placed.astype(BF16)
        offset += width


def assemble(blocks, order, widths):
    rank = blocks[0].shape[0]
    count = len(blocks)
    return pl.pallas_call(
        functools.partial(assemble_kernel, widths=widths, count=count),
        grid_spec=pltpu.PrefetchScalarGridSpec(
            num_scalar_prefetch=1,
            grid=(1,),
            in_specs=[whole(b.shape) for b in blocks],
            out_specs=[whole((rank, w * count)) for w in widths],
        ),
        out_shape=[jax.ShapeDtypeStruct((rank, w * count), BF16) for w in widths],
        compiler_params=params(8),
        name="assemble",
    )(jnp.stack(order).astype(jnp.int32), *blocks)


def attend_kernel(
    lengths_ref, q_ref, kv_ref, q_up, k_up, v_up, od_ref, cos_ref, sin_ref, *refs,
    parts, group, block, far,
):
    parts_refs = refs[:parts]
    keys_hbm, values_hbm, w_hbm, ctx_ref, pm_ref, out_ref = refs[parts : parts + 6]
    keys, values, weights, qs, nk, nv, cs, key_sems, value_sems, w_sems = refs[parts + 6 :]
    rows, dim = cos_ref.shape
    heads = q_ref.shape[1] // dim
    kv = heads // group
    rank = q_up.shape[0]
    scale = 1.0 / math.sqrt(dim)
    count = rows // block
    wide = weights.shape[0] * weights.shape[2]

    def cache_copy(source, target, sems, i):
        part = pl.ds(i * block, block)
        return pltpu.make_async_copy(source.at[part], target.at[part], sems.at[i])

    column = exchange(lax.axis_size("tp"))(lax.axis_index("tp"), far)
    tiles, _, size = weights.shape

    def w_copy(n):
        lane = pl.multiple_of(column * wide + n * size, size)
        return pltpu.make_async_copy(w_hbm.at[:, pl.ds(lane, size)], weights.at[n], w_sems.at[n])

    lead = min(2, count)
    for i in range(lead):
        cache_copy(keys_hbm, keys, key_sems, i).start()
        cache_copy(values_hbm, values, value_sems, i).start()

    total = parts_refs[0][...].astype(F32)
    for other in parts_refs[1:]:
        total += other[...].astype(F32)
    inner = total.astype(BF16)
    cosine, sine = cos_ref[...], sin_ref[...]

    def turned(x):
        return x * cosine + pltpu.roll(x, dim // 2, 1) * sine

    def delta(j, up):
        return adapter_scale * jnp.dot(
            inner[:, j * rank : (j + 1) * rank], up[...], preferred_element_type=F32
        )

    key_delta, value_delta, query_delta = delta(1, k_up), delta(2, v_up), delta(0, q_up)
    for g in range(kv):
        lane = slice(g * dim, (g + 1) * dim)
        key = turned(kv_ref[0, :, lane] + key_delta[:, lane]).astype(BF16).astype(F32)
        value = (kv_ref[1, :, lane] + value_delta[:, lane]).astype(BF16).astype(F32)
        for h in range(g * group, (g + 1) * group):
            lane = slice(h * dim, (h + 1) * dim)
            strided = pl.ds(h, rows, stride=heads)
            qs[strided, :] = turned(q_ref[:, lane] + query_delta[:, lane])
            nk[strided, :] = key
            nv[strided, :] = value

    row = lax.broadcasted_iota(jnp.int32, (heads, dim), 0)
    positions = keys.shape[2]
    spot = lax.broadcasted_iota(jnp.int32, (heads, positions), 1)

    def select(pieces):
        out = pieces[0]
        for g in range(1, kv):
            out = jnp.where(row >= g * group, pieces[g], out)
        return out

    def step(i, _):
        @pl.when(i + lead < count)
        def _():
            cache_copy(keys_hbm, keys, key_sems, i + lead).start()
            cache_copy(values_hbm, values, value_sems, i + lead).start()

        @pl.when(i + lead >= count)
        def _():
            for n in range(tiles):
                @pl.when(n * lead // tiles == i + lead - count)
                def _():
                    w_copy(n).start()

        cache_copy(keys_hbm, keys, key_sems, i).wait()
        span = pl.ds(pl.multiple_of(i * block * heads, block * heads), block * heads)
        query = qs[span, :]
        high = query.astype(BF16)
        rest = query - high.astype(F32)
        mid = rest.astype(BF16)
        low = (rest - mid.astype(F32)).astype(BF16)
        found = []
        for b in range(block):
            s = i * block + b
            at = slice(b * heads, (b + 1) * heads)
            q = jnp.concatenate([high[at], mid[at], low[at]], axis=0)
            pieces = []
            for g in range(kv):
                full = lax.dot_general(
                    q, keys[s, g], (((1,), (1,)), ((), ())), preferred_element_type=F32
                )
                pieces.append(full[:heads] + (full[heads : 2 * heads] + full[2 * heads :]))
            found.append(jnp.where(spot < lengths_ref[s], select(pieces) * scale, -1e30))
        scores = jnp.concatenate(found, axis=0)
        own_score = jnp.sum(query * nk[span, :], axis=-1, keepdims=True) * scale
        top = jnp.maximum(jnp.max(scores, axis=-1, keepdims=True), own_score)
        exps = jnp.exp(scores - top)
        own_weight = jnp.exp(own_score - top)
        denom = jnp.sum(exps, axis=-1, keepdims=True) + own_weight
        inverse = 1.0 / denom
        probs = (exps * inverse).astype(BF16)
        own_prob = (own_weight * inverse).astype(BF16).astype(F32)
        cache_copy(values_hbm, values, value_sems, i).wait()
        found = []
        for b in range(block):
            s = i * block + b
            p = probs[b * heads : (b + 1) * heads]
            pieces = [
                jnp.dot(p, values[s, g], preferred_element_type=F32) for g in range(kv)
            ]
            found.append(select(pieces))
        cs[span, :] = jnp.concatenate(found, axis=0) + own_prob * nv[span, :]
        return 0

    lax.fori_loop(0, count, step, 0)

    middle = jnp.zeros((rows, rank), F32)
    for h in range(heads):
        lane = slice(h * dim, (h + 1) * dim)
        context = cs[pl.ds(h, rows, stride=heads), :].astype(BF16)
        ctx_ref[:, lane] = context
        middle += lax.dot_general(
            context, od_ref[:, lane], (((1,), (1,)), ((), ())), preferred_element_type=F32
        )
    high = middle.astype(BF16)
    low = (middle - high.astype(F32)).astype(BF16)
    tail = jnp.concatenate([high, low], axis=1)
    pm_ref[...] = tail

    def project(n, _):
        w_copy(n).wait()
        lane = pl.ds(pl.multiple_of(n * size, size), size)
        part = jnp.dot(ctx_ref[...], weights[n], preferred_element_type=F32)
        out_ref[:, lane] = part.astype(BF16)
        return 0

    lax.fori_loop(0, tiles, project, 0)
    out_ref[:, wide:] = tail


def attention(lengths, base_q, base_kv, parts, ups, od, angles, keys, values, weights, far):
    rows, kv, positions, dim = keys.shape
    q_cols = base_q.shape[1]
    heads = q_cols // dim
    rank = od.shape[0]
    block = 16 if rows % 16 == 0 else rows
    wide = weights.shape[1] // lax.axis_size("tp")
    size = 512 if wide % 512 == 0 else wide
    vmem = pl.BlockSpec(memory_space=pltpu.VMEM)
    hbm = pl.BlockSpec(memory_space=pltpu.HBM)
    fixed = [base_q, base_kv] + list(ups) + [od] + list(angles) + list(parts)
    scratch = pltpu.VMEM((rows * heads, dim), F32)
    return pl.pallas_call(
        functools.partial(
            attend_kernel, parts=len(parts), group=heads // kv, block=block, far=far
        ),
        in_specs=[pl.BlockSpec(memory_space=pltpu.SMEM)] + [vmem] * len(fixed) + [hbm] * 3,
        out_specs=[vmem, vmem, vmem],
        scratch_shapes=[
            pltpu.VMEM(keys.shape, BF16),
            pltpu.VMEM(values.shape, BF16),
            pltpu.VMEM((wide // size, weights.shape[0], size), BF16),
            scratch,
            scratch,
            scratch,
            scratch,
            pltpu.SemaphoreType.DMA((rows // block,)),
            pltpu.SemaphoreType.DMA((rows // block,)),
            pltpu.SemaphoreType.DMA((wide // size,)),
        ],
        out_shape=[
            jax.ShapeDtypeStruct((rows, q_cols), BF16),
            jax.ShapeDtypeStruct((rows, 2 * rank), BF16),
            jax.ShapeDtypeStruct((rows, wide + 2 * rank), BF16),
        ],
        compiler_params=params(52),
        cost_estimate=pl.CostEstimate(
            flops=4 * rows * heads * positions * dim * 16,
            bytes_accessed=4 * keys.size,
            transcendentals=rows * heads * positions,
        ),
        name="attend",
    )(lengths, *fixed, keys, values, weights)


def chunk_kernel(ctx_ref, w_hbm, pm_ref, out_ref, held, sems, *, k):
    tiles, _, size = held.shape
    wide = tiles * size
    column = exchange(lax.axis_size("tp"))(lax.axis_index("tp"), k)

    def copy(n):
        lane = pl.multiple_of(column * wide + n * size, size)
        return pltpu.make_async_copy(w_hbm.at[:, pl.ds(lane, size)], held.at[n], sems.at[n])

    for n in range(tiles):
        copy(n).start()

    def project(n, _):
        copy(n).wait()
        lane = pl.ds(pl.multiple_of(n * size, size), size)
        part = jnp.dot(ctx_ref[...], held[n], preferred_element_type=F32)
        out_ref[:, lane] = part.astype(out_ref.dtype)
        return 0

    lax.fori_loop(0, tiles, project, 0)
    if k:
        out_ref[:, wide:] = pm_ref[...]


def chunk(context, weights, middle, k):
    rows, depth = context.shape
    wide = weights.shape[1] // lax.axis_size("tp")
    size = 512 if wide % 512 == 0 else wide
    tail = middle.shape[1] if k else 0
    vmem = pl.BlockSpec(memory_space=pltpu.VMEM)
    return pl.pallas_call(
        functools.partial(chunk_kernel, k=k),
        in_specs=[vmem, pl.BlockSpec(memory_space=pltpu.HBM), vmem],
        out_specs=vmem,
        out_shape=jax.ShapeDtypeStruct((rows, wide + tail), BF16 if k else F32),
        scratch_shapes=[
            pltpu.VMEM((wide // size, depth, size), BF16),
            pltpu.SemaphoreType.DMA((wide // size,)),
        ],
        compiler_params=params(52),
        cost_estimate=pl.CostEstimate(
            flops=2 * rows * depth * wide, bytes_accessed=2 * depth * wide, transcendentals=0
        ),
    )(context, weights, middle)


def final_kernel(own_ref, pm_ref, up_ref, *refs):
    others, out_ref = refs[:-1], refs[-1]
    wide = own_ref.shape[1]
    rank = up_ref.shape[0]
    total = own_ref[...]
    middle = pm_ref[:, :rank].astype(F32) + pm_ref[:, rank:].astype(F32)
    for other in others:
        total += other[:, :wide].astype(F32)
        tail = other[:, wide:].astype(F32)
        middle += tail[:, :rank] + tail[:, rank:]
    total += adapter_scale * jnp.dot(
        middle.astype(BF16), up_ref[...], preferred_element_type=F32
    )
    out_ref[...] = total.astype(BF16)


def finish(own, middle, out_up, others):
    args = [own, middle, out_up] + others
    return pl.pallas_call(
        final_kernel,
        grid=(1,),
        in_specs=[whole(a.shape) for a in args],
        out_specs=whole(own.shape),
        out_shape=jax.ShapeDtypeStruct(own.shape, BF16),
        compiler_params=params(8),
        name="final",
    )(*args)


def local(
    hidden,
    norm_gain,
    query_weight_matrix,
    key_value_weight,
    output_weight_matrix,
    input_down_factors,
    query_up_factor,
    key_value_up_factors,
    output_down_factor,
    output_up_factor,
    cache_keys,
    cache_values,
    lengths,
):
    rep = lax.axis_size("rep")
    tp = lax.axis_size("tp")
    t = lax.axis_index("tp")

    head_dim = cache_keys.shape[3]
    count, deep, rank = input_down_factors.shape
    down = input_down_factors.transpose(0, 2, 1).reshape(count * rank, deep)
    down_blocks, down_order = gather_rep(down)
    up_pack, widths = pack(
        query_up_factor, output_down_factor, output_up_factor, key_value_up_factors
    )
    moved = lax.ppermute(
        up_pack, ("rep", "tp"), [(b, (b % rep) * tp + b // rep) for b in range(rep * tp)]
    )
    normed, cosine, sine, base_q, base_kv = base_projections(
        hidden, norm_gain, lengths, query_weight_matrix, key_value_weight, head_dim
    )
    moved, base_q = lax.optimization_barrier((moved, base_q))
    up_blocks, up_order = gather_rep(moved)
    part = partial_inner(normed, down_blocks, [o * tp + t for o in down_order])
    parts = [part] + [hop(part, "tp", k) for k in range(1, tp)]
    q_up, od, out_up, k_up, v_up = assemble(up_blocks, up_order, widths)
    far = tp - 1
    context, middle, piece = attention(
        lengths, base_q, base_kv, parts, (q_up, k_up, v_up), od, (cosine, sine),
        cache_keys, cache_values, output_weight_matrix, far,
    )
    others = [hop(piece, "tp", far)]
    for k in range(far - 1, 0, -1):
        piece = chunk(context, output_weight_matrix, middle, k)
        others.append(hop(piece, "tp", k))
    own = chunk(context, output_weight_matrix, middle, 0)
    return finish(own, middle, out_up, others)


def solution(mesh):
    return jax.shard_map(
        local,
        mesh=mesh,
        in_specs=(
            P("rep", None),
            P(),
            P(None, "tp"),
            P(None, None, "tp"),
            P("tp", None),
            P(None, ("rep", "tp"), None),
            P(None, ("rep", "tp")),
            P(None, None, ("rep", "tp")),
            P(("rep", "tp"), None),
            P(None, ("rep", "tp")),
            P("rep", "tp", None, None),
            P("rep", "tp", None, None),
            P("rep"),
        ),
        out_specs=P("rep", "tp"),
        check_vma=False,
    )
```

profile of v0, /device:TPU:12, one launch (start us, length us, event | category | flops | bytes accessed | tf_op | source)
XLA Modules:
  0.0 80.0 jit_solution(856488639788815772)
XLA Ops:
  0.0 0.0 collective-permute-start.11
  0.0 1.4 %collective-permute-start.10 = (bf16[192,256]{1,0:T(8,128)(2,1)}, bf16[192,256]{1,0:T(8,128)(2,1)S(1)}, u32[]{:S(2)}, u32[]{:S(2)}) collective-permute-start(bf16[192,256]{1,0:T(8,128)(2,1)} %bitcast.23), channel_id=1, source_target_pairs={{0,24},{4,28},{8,16},{12,20},{16,8},{20,12},{24,0},{28,4},{1,25},{... | collective-permute-start | bytes 294920 | tf_op jit(solution)/shard_map/ppermute | solution.py:40
  1.4 1.5 %collective-permute-start.9 = (bf16[192,256]{1,0:T(8,128)(2,1)}, bf16[192,256]{1,0:T(8,128)(2,1)S(1)}, u32[]{:S(2)}, u32[]{:S(2)}) collective-permute-start(bf16[192,256]{1,0:T(8,128)(2,1)} %bitcast.24), channel_id=1, source_target_pairs={{0,16},{4,20},{8,24},{12,28},{16,0},{20,4},{24,8},{28,12},{1,17},{... | collective-permute-start | bytes 294920 | tf_op jit(solution)/shard_map/ppermute | solution.py:40
  3.0 0.5 collective-permute-start.8
  3.5 1.5 %pack.1 = bf16[64,576]{1,0:T(8,128)(2,1)} custom-call(bf16[64,128]{1,0:T(8,128)(2,1)} %q_ref.1, bf16[64,128]{1,0:T(8,128)(2,1)} %bitcast.28, bf16[64,256]{1,0:T(8,128)(2,1)} %ou_ref.1, bf16[2,32,64]{2,1,0:T(8,128)(2,1)} %bitcast.29), custom_call_target="tpu_custom_call" | custom-call | tf_op jit(solution)/shard_map/pack/pallas_call | solution.py:74
  5.0 2.7 %collective-permute-start = (bf16[64,576]{1,0:T(8,128)(2,1)}, bf16[64,576]{1,0:T(8,128)(2,1)S(1)}, u32[]{:S(2)}, u32[]{:S(2)}) collective-permute-start(bf16[64,576]{1,0:T(8,128)(2,1)} %pack.1), channel_id=1, source_target_pairs={{0,0},{1,4},{2,8},{3,12},{4,16},{5,20},{6,24},{7,28},{8,1},{9,5},{... | collective-permute-start | bytes 221192 | tf_op jit(solution)/shard_map/ppermute | solution.py:571
  7.7 0.0 copy-start.1
  7.7 0.6 copy-done.1
  8.4 0.0 copy-start.3
  8.4 0.7 copy-done.3
  9.1 0.0 copy-start
  9.1 0.0 copy-start.2
  9.1 12.4 %base.1 = (bf16[64,8192]{1,0:T(8,128)(2,1)S(1)}, f32[64,128]{1,0:T(8,128)S(1)}, f32[64,128]{1,0:T(8,128)S(1)}, f32[64,1024]{1,0:T(8,128)S(1)}, f32[2,64,256]{2,1,0:T(8,128)S(1)}) custom-call(s32[64]{0:T(128)S(1)} %copy-done.1, bf16[64,128]{1,0:T(8,128)(2,1)S(1)} %bitcast.27, bf16[64,8192]{1,0:T(8,128)(2,1)} %hidden_hbm.1, bf16[8192,1024]{1,0:T(8,128)(2,1)} %q_hbm.1, ...), custom_call_target="tpu_custom_call" | custom-call | flops 12884901888 | bytes 25165824 | tf_op jit(solution)/shard_map/base/pallas_call | solution.py:165
  21.5 0.0 collective-permute-done.refs_0_
  21.5 0.7 collective-permute-start.3
  22.2 0.0 collective-permute-done.11.refs_4_
  22.2 3.3 %collective-permute-start.2 = (bf16[64,576]{1,0:T(8,128)(2,1)S(1)}, bf16[64,576]{1,0:T(8,128)(2,1)S(1)}, u32[]{:S(2)}, u32[]{:S(2)}) collective-permute-start(bf16[64,576]{1,0:T(8,128)(2,1)S(1)} %collective-permute-done.refs_0_), channel_id=1, source_target_pairs={{0,16},{4,20},{8,24},{12,28},{16,0},{20,4},{24,8},{28,12},{1,17},{... | collective-permute-start | bytes 221192 | tf_op jit(solution)/shard_map/ppermute | solution.py:40
  25.5 0.0 collective-permute-done.10.refs_3_
  25.5 0.0 collective-permute-start.1
  25.5 0.0 collective-permute-done.9.refs_2_
  25.5 0.1 collective-permute-start.14
  25.6 0.0 collective-permute-done.8.refs_1_
  25.6 0.5 collective-permute-start.13
  26.1 1.0 %collective-permute-done.3.refs_3_ = bf16[64,576]{1,0:T(8,128)(2,1)S(1)} collective-permute-done((bf16[64,576]{1,0:T(8,128)(2,1)S(1)}, bf16[64,576]{1,0:T(8,128)(2,1)S(1)}, u32[]{:S(2)}, u32[]{:S(2)}) %collective-permute-start.3) | collective-permute-done | bytes 73760 | tf_op jit(solution)/shard_map/ppermute | solution.py:40
  27.1 0.0 collective-permute-start.12
  27.1 1.7 %collective-permute-done.2.refs_2_ = bf16[64,576]{1,0:T(8,128)(2,1)S(1)} collective-permute-done((bf16[64,576]{1,0:T(8,128)(2,1)S(1)}, bf16[64,576]{1,0:T(8,128)(2,1)S(1)}, u32[]{:S(2)}, u32[]{:S(2)}) %collective-permute-start.2) | collective-permute-done | bytes 73760 | tf_op jit(solution)/shard_map/ppermute | solution.py:40
  28.8 0.0 collective-permute-start.4
  28.8 1.2 %collective-permute-done.1.refs_1_ = bf16[64,576]{1,0:T(8,128)(2,1)S(1)} collective-permute-done((bf16[64,576]{1,0:T(8,128)(2,1)S(1)}, bf16[64,576]{1,0:T(8,128)(2,1)S(1)}, u32[]{:S(2)}, u32[]{:S(2)}) %collective-permute-start.1) | collective-permute-done | bytes 73760 | tf_op jit(solution)/shard_map/ppermute | solution.py:40
  30.0 0.0 collective-permute-start.7
  30.0 0.0 collective-permute-done.14.refs_7_
  30.0 0.5 collective-permute-start.6
  30.5 0.0 collective-permute-done.13.refs_6_
  30.5 0.1 collective-permute-start.5
  30.6 0.1 stack.71.starts_ref
  30.6 0.0 collective-permute-done.12.refs_5_
  30.6 0.0 copy-done
  30.7 0.9 %inner.1.refs_0_ = bf16[64,256]{1,0:T(8,128)(2,1)S(1)} custom-call(s32[8]{0:T(128)S(1)} %stack.71.starts_ref, bf16[64,8192]{1,0:T(8,128)(2,1)S(1)} %get-tuple-element.30.x_ref, bf16[192,256]{1,0:T(8,128)(2,1)S(1)} %bitcast.26, bf16[192,256]{1,0:T(8,128)(2,1)S(1)} %collective-permute-done.8.refs_1_, bf16[192,256]{1,0:T(8,128)(2,1)S(1)} %collective-permute-done.9.refs_2_, ...), custom_call_target="tpu_custom_call" | custom-call | flops 50331648 | bytes 786432 | tf_op jit(solution)/shard_map/inner/pallas_call | solution.py:216
  31.6 1.5 %collective-permute-start.17 = (bf16[64,256]{1,0:T(8,128)(2,1)S(1)}, bf16[64,256]{1,0:T(8,128)(2,1)S(1)}, u32[]{:S(2)}, u32[]{:S(2)}) collective-permute-start(bf16[64,256]{1,0:T(8,128)(2,1)S(1)} %inner.1.refs_0_), channel_id=1, source_target_pairs={{0,3},{1,2},{2,1},{3,0},{4,7},{5,6},{6,5},{7,4},{8,11},{9,10},{10,... | collective-permute-start | bytes 98312 | tf_op jit(solution)/shard_map/ppermute | solution.py:40
  33.1 0.0 collective-permute-done.4.refs_4_
  33.1 3.1 %collective-permute-start.16 = (bf16[64,256]{1,0:T(8,128)(2,1)S(1)}, bf16[64,256]{1,0:T(8,128)(2,1)S(1)}, u32[]{:S(2)}, u32[]{:S(2)}) collective-permute-start(bf16[64,256]{1,0:T(8,128)(2,1)S(1)} %inner.1.refs_0_), channel_id=1, source_target_pairs={{0,2},{1,3},{2,0},{3,1},{4,6},{5,7},{6,4},{7,5},{8,10},{9,11},{10,... | collective-permute-start | bytes 98312 | tf_op jit(solution)/shard_map/ppermute | solution.py:40
  36.2 0.0 collective-permute-done.7.refs_7_
  36.2 0.0 collective-permute-start.15
  36.2 0.1 stack.62.order_ref
  36.3 0.0 collective-permute-done.6.refs_6_
  36.3 0.0 collective-permute-done.5.refs_5_
  36.3 0.9 %assemble.1 = (bf16[64,1024]{1,0:T(8,128)(2,1)S(1)}, bf16[64,1024]{1,0:T(8,128)(2,1)S(1)}, bf16[64,2048]{1,0:T(8,128)(2,1)S(1)}, bf16[64,256]{1,0:T(8,128)(2,1)S(1)}, bf16[64,256]{1,0:T(8,128)(2,1)S(1)}) custom-call(s32[8]{0:T(128)S(1)} %stack.62.order_ref, bf16[64,576]{1,0:T(8,128)(2,1)S(1)} %collective-permute-done.refs_0_, ...), custom_call_target="tpu_custom_call" | custom-call | tf_op jit(solution)/shard_map/assemble/pallas_call | solution.py:265
  37.2 0.0 collective-permute-done.17.refs_3_
  37.2 1.7 %collective-permute-done.16.refs_2_ = bf16[64,256]{1,0:T(8,128)(2,1)S(1)} collective-permute-done((bf16[64,256]{1,0:T(8,128)(2,1)S(1)}, bf16[64,256]{1,0:T(8,128)(2,1)S(1)}, u32[]{:S(2)}, u32[]{:S(2)}) %collective-permute-start.16) | collective-permute-done | bytes 32800 | tf_op jit(solution)/shard_map/ppermute | solution.py:40
  38.9 1.2 %collective-permute-done.15.refs_1_ = bf16[64,256]{1,0:T(8,128)(2,1)S(1)} collective-permute-done((bf16[64,256]{1,0:T(8,128)(2,1)S(1)}, bf16[64,256]{1,0:T(8,128)(2,1)S(1)}, u32[]{:S(2)}, u32[]{:S(2)}) %collective-permute-start.15) | collective-permute-done | bytes 32800 | tf_op jit(solution)/shard_map/ppermute | solution.py:40
  40.1 0.0 copy-done.2
  40.1 8.2 %attend.1 = (bf16[64,1024]{1,0:T(8,128)(2,1)S(1)}, bf16[64,128]{1,0:T(8,128)(2,1)S(1)}, bf16[64,2176]{1,0:T(8,128)(2,1)S(1)}) custom-call(s32[64]{0:T(128)S(1)} %copy-done.2, f32[64,1024]{1,0:T(8,128)S(1)} %get-tuple-element.21.q_ref, f32[2,64,256]{2,1,0:T(8,128)S(1)} %get-tuple-element.22.kv_ref, bf16[64,1024]{1,0:T(8,128)(2,1)S(1)} %get-tuple-element.24.q_up, ...), custom_call_target="tpu_custom_call" | custom-call | flops 536870912 | bytes 8388608 | tf_op jit(solution)/shard_map/attend/pallas_call | solution.py:437
  48.4 2.5 %shard_map.129 = bf16[64,2176]{1,0:T(8,128)(2,1)S(1)} custom-call(bf16[64,1024]{1,0:T(8,128)(2,1)S(1)} %get-tuple-element.31.ctx_ref, bf16[1024,8192]{1,0:T(8,128)(2,1)} %w_hbm.5, bf16[64,128]{1,0:T(8,128)(2,1)S(1)} %get-tuple-element.32.pm_ref), custom_call_target="tpu_custom_call" | custom-call | flops 268435456 | bytes 4194304 | tf_op jit(solution)/shard_map/pallas_call | solution.py:500
  50.9 2.5 %shard_map.128 = bf16[64,2176]{1,0:T(8,128)(2,1)S(1)} custom-call(bf16[64,1024]{1,0:T(8,128)(2,1)S(1)} %get-tuple-element.31.ctx_ref, bf16[1024,8192]{1,0:T(8,128)(2,1)} %w_hbm.5, bf16[64,128]{1,0:T(8,128)(2,1)S(1)} %get-tuple-element.32.pm_ref), custom_call_target="tpu_custom_call" | custom-call | flops 268435456 | bytes 4194304 | tf_op jit(solution)/shard_map/pallas_call | solution.py:500
  53.5 1.0 %collective-permute-start.19 = (bf16[64,2176]{1,0:T(8,128)(2,1)S(1)}, bf16[64,2176]{1,0:T(8,128)(2,1)S(1)}, u32[]{:S(2)}, u32[]{:S(2)}) collective-permute-start(bf16[64,2176]{1,0:T(8,128)(2,1)S(1)} %shard_map.128), channel_id=1, source_target_pairs={{0,2},{1,3},{2,0},{3,1},{4,6},{5,7},{6,4},{7,5},{8,10},{9,11},{10,... | collective-permute-start | bytes 835592 | tf_op jit(solution)/shard_map/ppermute | solution.py:40
  54.4 0.6 collective-permute-start.20
  55.0 2.0 %collective-permute-start.18 = (bf16[64,2176]{1,0:T(8,128)(2,1)S(1)}, bf16[64,2176]{1,0:T(8,128)(2,1)S(1)}, u32[]{:S(2)}, u32[]{:S(2)}) collective-permute-start(bf16[64,2176]{1,0:T(8,128)(2,1)S(1)} %get-tuple-element.34), channel_id=1, source_target_pairs={{0,3},{1,2},{2,1},{3,0},{4,7},{5,6},{6,5},{7,4},{8,11},{9,10},{10,... | collective-permute-start | bytes 835592 | tf_op jit(solution)/shard_map/ppermute | solution.py:40
  57.0 2.5 %shard_map.127.own_ref = f32[64,2048]{1,0:T(8,128)S(1)} custom-call(bf16[64,1024]{1,0:T(8,128)(2,1)S(1)} %get-tuple-element.31.ctx_ref, bf16[1024,8192]{1,0:T(8,128)(2,1)} %w_hbm.5, bf16[64,128]{1,0:T(8,128)(2,1)S(1)} %get-tuple-element.32.pm_ref), custom_call_target="tpu_custom_call" | custom-call | flops 268435456 | bytes 4194304 | tf_op jit(solution)/shard_map/pallas_call | solution.py:500
  59.5 7.8 %collective-permute-done.19.refs_1_ = bf16[64,2176]{1,0:T(8,128)(2,1)S(1)} collective-permute-done((bf16[64,2176]{1,0:T(8,128)(2,1)S(1)}, bf16[64,2176]{1,0:T(8,128)(2,1)S(1)}, u32[]{:S(2)}, u32[]{:S(2)}) %collective-permute-start.19) | collective-permute-done | bytes 278560 | tf_op jit(solution)/shard_map/ppermute | solution.py:40
  67.3 1.2 %collective-permute-done.20.refs_2_ = bf16[64,2176]{1,0:T(8,128)(2,1)S(1)} collective-permute-done((bf16[64,2176]{1,0:T(8,128)(2,1)S(1)}, bf16[64,2176]{1,0:T(8,128)(2,1)S(1)}, u32[]{:S(2)}, u32[]{:S(2)}) %collective-permute-start.20) | collective-permute-done | bytes 278560 | tf_op jit(solution)/shard_map/ppermute | solution.py:40
  68.5 10.5 %collective-permute-done.18.refs_0_ = bf16[64,2176]{1,0:T(8,128)(2,1)S(1)} collective-permute-done((bf16[64,2176]{1,0:T(8,128)(2,1)S(1)}, bf16[64,2176]{1,0:T(8,128)(2,1)S(1)}, u32[]{:S(2)}, u32[]{:S(2)}) %collective-permute-start.18) | collective-permute-done | bytes 278560 | tf_op jit(solution)/shard_map/ppermute | solution.py:40
  79.0 1.0 %final.1 = bf16[64,2048]{1,0:T(8,128)(2,1)} custom-call(f32[64,2048]{1,0:T(8,128)S(1)} %shard_map.127.own_ref, bf16[64,128]{1,0:T(8,128)(2,1)S(1)} %get-tuple-element.32.pm_ref, bf16[64,2048]{1,0:T(8,128)(2,1)S(1)} %get-tuple-element.33.up_ref, bf16[64,2176]{1,0:T(8,128)(2,1)S(1)} %collective-permute-done.18.refs_0_, ...), custom_call_target="tpu_custom_call" | custom-call | tf_op jit(solution)/shard_map/final/pallas_call | solution.py:534
Async XLA Ops:
  0.0 22.2 %collective-permute-start.11 = (bf16[192,256]{1,0:T(8,128)(2,1)}, bf16[192,256]{1,0:T(8,128)(2,1)S(1)}, u32[]{:S(2)}, u32[]{:S(2)}) collective-permute-start(bf16[192,256]{1,0:T(8,128)(2,1)} %bitcast.22), channel_id=1, source_target_pairs={{0,4},{4,0},{8,12},{12,8},{16,20},{20,16},{24,28},{28,24},{1,5},{5... | collective-permute-start | bytes 294920 | tf_op jit(solution)/shard_map/ppermute | solution.py:40
  0.0 25.5 %collective-permute-start.10 = (bf16[192,256]{1,0:T(8,128)(2,1)}, bf16[192,256]{1,0:T(8,128)(2,1)S(1)}, u32[]{:S(2)}, u32[]{:S(2)}) collective-permute-start(bf16[192,256]{1,0:T(8,128)(2,1)} %bitcast.23), channel_id=1, source_target_pairs={{0,24},{4,28},{8,16},{12,20},{16,8},{20,12},{24,0},{28,4},{1,25},{... | collective-permute-start | bytes 294920 | tf_op jit(solution)/shard_map/ppermute | solution.py:40
  1.4 24.1 %collective-permute-start.9 = (bf16[192,256]{1,0:T(8,128)(2,1)}, bf16[192,256]{1,0:T(8,128)(2,1)S(1)}, u32[]{:S(2)}, u32[]{:S(2)}) collective-permute-start(bf16[192,256]{1,0:T(8,128)(2,1)} %bitcast.24), channel_id=1, source_target_pairs={{0,16},{4,20},{8,24},{12,28},{16,0},{20,4},{24,8},{28,12},{1,17},{... | collective-permute-start | bytes 294920 | tf_op jit(solution)/shard_map/ppermute | solution.py:40
  3.0 22.7 %collective-permute-start.8 = (bf16[192,256]{1,0:T(8,128)(2,1)}, bf16[192,256]{1,0:T(8,128)(2,1)S(1)}, u32[]{:S(2)}, u32[]{:S(2)}) collective-permute-start(bf16[192,256]{1,0:T(8,128)(2,1)} %bitcast.25), channel_id=1, source_target_pairs={{0,8},{4,12},{8,0},{12,4},{16,24},{20,28},{24,16},{28,20},{1,9},{5... | collective-permute-start | bytes 294920 | tf_op jit(solution)/shard_map/ppermute | solution.py:40
  5.0 16.5 %collective-permute-start = (bf16[64,576]{1,0:T(8,128)(2,1)}, bf16[64,576]{1,0:T(8,128)(2,1)S(1)}, u32[]{:S(2)}, u32[]{:S(2)}) collective-permute-start(bf16[64,576]{1,0:T(8,128)(2,1)} %pack.1), channel_id=1, source_target_pairs={{0,0},{1,4},{2,8},{3,12},{4,16},{5,20},{6,24},{7,28},{8,1},{9,5},{... | collective-permute-start | bytes 221192 | tf_op jit(solution)/shard_map/ppermute | solution.py:571
  7.7 0.7 copy-start.1
  8.4 0.7 copy-start.3
  9.1 21.6 %copy-start = (bf16[3,256,64]{1,2,0:T(8,128)(2,1)S(1)}, bf16[3,256,64]{1,2,0:T(8,128)(2,1)}, u32[]{:S(2)}) copy-start(bf16[3,256,64]{1,2,0:T(8,128)(2,1)} %param.18) | copy-start | bytes 294916
  9.1 31.0 %copy-start.2 = (s32[64]{0:T(128)S(1)}, s32[64]{0:T(128)}, u32[]{:S(2)}) copy-start(s32[64]{0:T(128)} %lengths_ref.3) | copy-start | bytes 772
  21.5 5.6 %collective-permute-start.3 = (bf16[64,576]{1,0:T(8,128)(2,1)S(1)}, bf16[64,576]{1,0:T(8,128)(2,1)S(1)}, u32[]{:S(2)}, u32[]{:S(2)}) collective-permute-start(bf16[64,576]{1,0:T(8,128)(2,1)S(1)} %collective-permute-done.refs_0_), channel_id=1, source_target_pairs={{0,24},{4,28},{8,16},{12,20},{16,8},{20,12},{24,0},{28,4},{1,25},{... | collective-permute-start | bytes 221192 | tf_op jit(solution)/shard_map/ppermute | solution.py:40
  22.2 6.5 %collective-permute-start.2 = (bf16[64,576]{1,0:T(8,128)(2,1)S(1)}, bf16[64,576]{1,0:T(8,128)(2,1)S(1)}, u32[]{:S(2)}, u32[]{:S(2)}) collective-permute-start(bf16[64,576]{1,0:T(8,128)(2,1)S(1)} %collective-permute-done.refs_0_), channel_id=1, source_target_pairs={{0,16},{4,20},{8,24},{12,28},{16,0},{20,4},{24,8},{28,12},{1,17},{... | collective-permute-start | bytes 221192 | tf_op jit(solution)/shard_map/ppermute | solution.py:40
  25.5 4.4 %collective-permute-start.1 = (bf16[64,576]{1,0:T(8,128)(2,1)S(1)}, bf16[64,576]{1,0:T(8,128)(2,1)S(1)}, u32[]{:S(2)}, u32[]{:S(2)}) collective-permute-start(bf16[64,576]{1,0:T(8,128)(2,1)S(1)} %collective-permute-done.refs_0_), channel_id=1, source_target_pairs={{0,8},{4,12},{8,0},{12,4},{16,24},{20,28},{24,16},{28,20},{1,9},{5... | collective-permute-start | bytes 221192 | tf_op jit(solution)/shard_map/ppermute | solution.py:40
  25.5 4.4 %collective-permute-start.14 = (bf16[192,256]{1,0:T(8,128)(2,1)S(1)}, bf16[192,256]{1,0:T(8,128)(2,1)S(1)}, u32[]{:S(2)}, u32[]{:S(2)}) collective-permute-start(bf16[192,256]{1,0:T(8,128)(2,1)S(1)} %collective-permute-done.10.refs_3_), channel_id=1, source_target_pairs={{0,4},{4,0},{8,12},{12,8},{16,20},{20,16},{24,28},{28,24},{1,5},{5... | collective-permute-start | bytes 294920 | tf_op jit(solution)/shard_map/ppermute | solution.py:40
  25.6 4.9 %collective-permute-start.13 = (bf16[192,256]{1,0:T(8,128)(2,1)S(1)}, bf16[192,256]{1,0:T(8,128)(2,1)S(1)}, u32[]{:S(2)}, u32[]{:S(2)}) collective-permute-start(bf16[192,256]{1,0:T(8,128)(2,1)S(1)} %collective-permute-done.9.refs_2_), channel_id=1, source_target_pairs={{0,4},{4,0},{8,12},{12,8},{16,20},{20,16},{24,28},{28,24},{1,5},{5... | collective-permute-start | bytes 294920 | tf_op jit(solution)/shard_map/ppermute | solution.py:40
  27.1 3.6 %collective-permute-start.12 = (bf16[192,256]{1,0:T(8,128)(2,1)S(1)}, bf16[192,256]{1,0:T(8,128)(2,1)S(1)}, u32[]{:S(2)}, u32[]{:S(2)}) collective-permute-start(bf16[192,256]{1,0:T(8,128)(2,1)S(1)} %collective-permute-done.8.refs_1_), channel_id=1, source_target_pairs={{0,4},{4,0},{8,12},{12,8},{16,20},{20,16},{24,28},{28,24},{1,5},{5... | collective-permute-start | bytes 294920 | tf_op jit(solution)/shard_map/ppermute | solution.py:40
  28.8 4.3 %collective-permute-start.4 = (bf16[64,576]{1,0:T(8,128)(2,1)S(1)}, bf16[64,576]{1,0:T(8,128)(2,1)S(1)}, u32[]{:S(2)}, u32[]{:S(2)}) collective-permute-start(bf16[64,576]{1,0:T(8,128)(2,1)S(1)} %collective-permute-done.refs_0_), channel_id=1, source_target_pairs={{0,4},{4,0},{8,12},{12,8},{16,20},{20,16},{24,28},{28,24},{1,5},{5... | collective-permute-start | bytes 221192 | tf_op jit(solution)/shard_map/ppermute | solution.py:40
  30.0 6.2 %collective-permute-start.7 = (bf16[64,576]{1,0:T(8,128)(2,1)S(1)}, bf16[64,576]{1,0:T(8,128)(2,1)S(1)}, u32[]{:S(2)}, u32[]{:S(2)}) collective-permute-start(bf16[64,576]{1,0:T(8,128)(2,1)S(1)} %collective-permute-done.3.refs_3_), channel_id=1, source_target_pairs={{0,4},{4,0},{8,12},{12,8},{16,20},{20,16},{24,28},{28,24},{1,5},{5... | collective-permute-start | bytes 221192 | tf_op jit(solution)/shard_map/ppermute | solution.py:40
  30.0 6.3 %collective-permute-start.6 = (bf16[64,576]{1,0:T(8,128)(2,1)S(1)}, bf16[64,576]{1,0:T(8,128)(2,1)S(1)}, u32[]{:S(2)}, u32[]{:S(2)}) collective-permute-start(bf16[64,576]{1,0:T(8,128)(2,1)S(1)} %collective-permute-done.2.refs_2_), channel_id=1, source_target_pairs={{0,4},{4,0},{8,12},{12,8},{16,20},{20,16},{24,28},{28,24},{1,5},{5... | collective-permute-start | bytes 221192 | tf_op jit(solution)/shard_map/ppermute | solution.py:40
  30.5 5.8 %collective-permute-start.5 = (bf16[64,576]{1,0:T(8,128)(2,1)S(1)}, bf16[64,576]{1,0:T(8,128)(2,1)S(1)}, u32[]{:S(2)}, u32[]{:S(2)}) collective-permute-start(bf16[64,576]{1,0:T(8,128)(2,1)S(1)} %collective-permute-done.1.refs_1_), channel_id=1, source_target_pairs={{0,4},{4,0},{8,12},{12,8},{16,20},{20,16},{24,28},{28,24},{1,5},{5... | collective-permute-start | bytes 221192 | tf_op jit(solution)/shard_map/ppermute | solution.py:40
  31.6 5.7 %collective-permute-start.17 = (bf16[64,256]{1,0:T(8,128)(2,1)S(1)}, bf16[64,256]{1,0:T(8,128)(2,1)S(1)}, u32[]{:S(2)}, u32[]{:S(2)}) collective-permute-start(bf16[64,256]{1,0:T(8,128)(2,1)S(1)} %inner.1.refs_0_), channel_id=1, source_target_pairs={{0,3},{1,2},{2,1},{3,0},{4,7},{5,6},{6,5},{7,4},{8,11},{9,10},{10,... | collective-permute-start | bytes 98312 | tf_op jit(solution)/shard_map/ppermute | solution.py:40
  33.1 5.9 %collective-permute-start.16 = (bf16[64,256]{1,0:T(8,128)(2,1)S(1)}, bf16[64,256]{1,0:T(8,128)(2,1)S(1)}, u32[]{:S(2)}, u32[]{:S(2)}) collective-permute-start(bf16[64,256]{1,0:T(8,128)(2,1)S(1)} %inner.1.refs_0_), channel_id=1, source_target_pairs={{0,2},{1,3},{2,0},{3,1},{4,6},{5,7},{6,4},{7,5},{8,10},{9,11},{10,... | collective-permute-start | bytes 98312 | tf_op jit(solution)/shard_map/ppermute | solution.py:40
  36.2 3.9 %collective-permute-start.15 = (bf16[64,256]{1,0:T(8,128)(2,1)S(1)}, bf16[64,256]{1,0:T(8,128)(2,1)S(1)}, u32[]{:S(2)}, u32[]{:S(2)}) collective-permute-start(bf16[64,256]{1,0:T(8,128)(2,1)S(1)} %inner.1.refs_0_), channel_id=1, source_target_pairs={{0,1},{1,0},{2,3},{3,2},{4,5},{5,4},{6,7},{7,6},{8,9},{9,8},{10,11... | collective-permute-start | bytes 98312 | tf_op jit(solution)/shard_map/ppermute | solution.py:40
  53.5 13.8 %collective-permute-start.19 = (bf16[64,2176]{1,0:T(8,128)(2,1)S(1)}, bf16[64,2176]{1,0:T(8,128)(2,1)S(1)}, u32[]{:S(2)}, u32[]{:S(2)}) collective-permute-start(bf16[64,2176]{1,0:T(8,128)(2,1)S(1)} %shard_map.128), channel_id=1, source_target_pairs={{0,2},{1,3},{2,0},{3,1},{4,6},{5,7},{6,4},{7,5},{8,10},{9,11},{10,... | collective-permute-start | bytes 835592 | tf_op jit(solution)/shard_map/ppermute | solution.py:40
  54.4 14.0 %collective-permute-start.20 = (bf16[64,2176]{1,0:T(8,128)(2,1)S(1)}, bf16[64,2176]{1,0:T(8,128)(2,1)S(1)}, u32[]{:S(2)}, u32[]{:S(2)}) collective-permute-start(bf16[64,2176]{1,0:T(8,128)(2,1)S(1)} %shard_map.129), channel_id=1, source_target_pairs={{0,1},{1,0},{2,3},{3,2},{4,5},{5,4},{6,7},{7,6},{8,9},{9,8},{10,11... | collective-permute-start | bytes 835592 | tf_op jit(solution)/shard_map/ppermute | solution.py:40
  55.0 24.0 %collective-permute-start.18 = (bf16[64,2176]{1,0:T(8,128)(2,1)S(1)}, bf16[64,2176]{1,0:T(8,128)(2,1)S(1)}, u32[]{:S(2)}, u32[]{:S(2)}) collective-permute-start(bf16[64,2176]{1,0:T(8,128)(2,1)S(1)} %get-tuple-element.34), channel_id=1, source_target_pairs={{0,3},{1,2},{2,1},{3,0},{4,7},{5,6},{6,5},{7,4},{8,11},{9,10},{10,... | collective-permute-start | bytes 835592 | tf_op jit(solution)/shard_map/ppermute | solution.py:40
where the time goes:
time: 80.4 us; the launch traced here: 80 us
  Pallas kernels  32.6 us (41%)
  waiting for transfers between devices  26.2 us (33%)
  starting transfers between devices  19.5 us (24%)
  local copies, waits for them, and re-layouts  1.54 us (2%)
    ppermute x20, waiting for transfers between devices, hop(): return lax.ppermute(x, axis, [(i, to(i, k)) for i in range(n)])  26.2 us
    ppermute x20, starting transfers between devices, hop(): return lax.ppermute(x, axis, [(i, to(i, k)) for i in range(n)])  16.9 us
    pallas_call x1, Pallas kernels, base_projections(): pl.pallas_call(base_kernel, in_specs=[pl.BlockSpec(memory_space=pltpu.SME...  12.4 us
    pallas_call x1, Pallas kernels, attention(): pl.pallas_call(functools.partial(attend_kernel, parts=len(parts), group=h...  8.24 us
    pallas_call x3, Pallas kernels, chunk(): pl.pallas_call(functools.partial(chunk_kernel, k=k), in_specs=[vmem, pl.B...  7.61 us
    ppermute x1, starting transfers between devices, local(): lax.ppermute(up_pack, ('rep', 'tp'), [(b, b % rep * tp + b // rep) for b...  2.69 us
  transfers between devices with their start and end apart: 21, of which 8 were waited for; matrix products, arithmetic and copies ran while one was open for 0% of the time, Pallas kernels for 23%

commit v1 on v0

v1 whole, which is shorter than its diff:
```python
import functools
import math

import jax
import jax.numpy as jnp
from jax import lax
from jax.experimental import pallas as pl
from jax.experimental.pallas import tpu as pltpu
from jax.sharding import PartitionSpec as P


epsilon = 1e-06
rope_base = 1000000.0
adapter_scale = 0.5
F32 = jnp.float32
BF16 = jnp.bfloat16


INNER = 6 * 10**9
LONG = pl.CostEstimate(flops=1 << 34, bytes_accessed=1 << 20, transcendentals=0)


def params(mib=24):
    return pltpu.CompilerParams(vmem_limit_bytes=mib * 1024 * 1024)


def whole(shape):
    return pl.BlockSpec(shape, lambda *_: (0,) * len(shape))


def power_of_two(n):
    return n & (n - 1) == 0


def exchange(n):
    if power_of_two(n):
        return lambda i, k: i ^ k
    return lambda i, k: (i + k) % n


def hop(x, axis, k):
    n = lax.axis_size(axis)
    to = exchange(n)
    return lax.ppermute(x, axis, [(i, to(i, k)) for i in range(n)])


def came_from(index, n, k):
    if power_of_two(n):
        return index ^ k
    return (index - k) % n


def gather_rep(block):
    n = lax.axis_size("rep")

    def sent(x, k):
        return hop(x, "rep", k)

    if not power_of_two(n) or n == 1:
        return [block] + [sent(block, k) for k in range(1, n)]
    near = [block] + [sent(block, k) for k in range(2, n, 2)]
    swapped = []
    for b in near:
        swapped.append(hop(b, "rep", 1))
    return near + swapped


def rep_order():
    n = lax.axis_size("rep")
    r = lax.axis_index("rep")
    if not power_of_two(n) or n == 1:
        return [came_from(r, n, k) for k in range(n)]
    return [r ^ k for k in range(0, n, 2)] + [r ^ k ^ 1 for k in range(0, n, 2)]


def pack_kernel(q_ref, od_ref, ou_ref, kv_ref, out_ref):
    both = jnp.concatenate([kv_ref[0], kv_ref[1]], axis=0).astype(F32).T.astype(BF16)
    lane = 0
    for piece in (q_ref[...], od_ref[...], ou_ref[...], both):
        out_ref[:, lane : lane + piece.shape[1]] = piece
        lane += piece.shape[1]


def pack(q_up, od, ou, kv_up):
    widths = (q_up.shape[1], od.shape[0], ou.shape[1], kv_up.shape[2], kv_up.shape[2])
    if any(w % 128 for w in widths[:3]):
        return jnp.concatenate([q_up, od.T, ou, kv_up[0], kv_up[1]], axis=1), widths
    vmem = pl.BlockSpec(memory_space=pltpu.VMEM)
    packed = pl.pallas_call(
        pack_kernel,
        in_specs=[vmem] * 4,
        out_specs=vmem,
        out_shape=jax.ShapeDtypeStruct((q_up.shape[0], sum(widths)), BF16),
        compiler_params=params(4),
        name="pack",
    )(q_up, od.T, ou, kv_up.transpose(0, 2, 1))
    return packed, widths


def opening_kernel(out_ref):
    out_ref[...] = jnp.zeros_like(out_ref)


def opening():
    return pl.pallas_call(
        opening_kernel,
        out_specs=pl.BlockSpec(memory_space=pltpu.VMEM),
        out_shape=jax.ShapeDtypeStruct((8, 128), F32),
        compiler_params=params(1),
        cost_estimate=LONG,
        name="opening",
    )()


def tables_kernel(lengths_ref, _, cos_ref, sin_ref, angle):
    rows = cos_ref.shape[0]
    dim = cos_ref.shape[1]
    spot = lax.broadcasted_iota(jnp.int32, (1, dim), 1) % (dim // 2)
    freq = jnp.ones((1, dim), F32)
    for bit in range((dim // 2 - 1).bit_length()):
        power = rope_base ** (-(2.0 ** (bit + 1)) / dim)
        freq *= jnp.where((spot >> bit) % 2 == 1, power, 1.0)
    for s in range(rows):
        angle[s : s + 1, :] = freq * lengths_ref[s].astype(F32)
    low = lax.broadcasted_iota(jnp.int32, (rows, dim), 1) < dim // 2
    wave = jnp.sin(angle[...] + jnp.where(low, 0.0, math.pi / 2))
    other = pltpu.roll(wave, dim // 2, 1)
    cos_ref[...] = jnp.where(low, other, wave)
    sin_ref[...] = jnp.where(low, -wave, other)


def tables(lengths, opened, dim):
    rows = lengths.shape[0]
    vmem = pl.BlockSpec(memory_space=pltpu.VMEM)
    return pl.pallas_call(
        tables_kernel,
        in_specs=[pl.BlockSpec(memory_space=pltpu.SMEM), vmem],
        out_specs=[vmem] * 2,
        out_shape=[jax.ShapeDtypeStruct((rows, dim), F32)] * 2,
        scratch_shapes=[pltpu.VMEM((rows, dim), F32)],
        compiler_params=params(4),
        name="tables",
    )(lengths, opened)


def base_kernel(gain_ref, hidden, q_held, kv_held, x_ref, q_out, kv_out):
    rows, wide = hidden.shape
    depth = 512

    q_out[...] = jnp.zeros_like(q_out)
    kv_out[...] = jnp.zeros_like(kv_out)

    part = gain_ref.shape[1]
    square = jnp.zeros((rows, part), F32)
    for j in range(wide // part):
        states = hidden[:, j * part : (j + 1) * part].astype(F32)
        square += states * states
    factor = lax.rsqrt(jnp.sum(square, axis=-1, keepdims=True) / wide + epsilon)
    for j in range(wide // part):
        lane = slice(j * part, (j + 1) * part)
        scaled = hidden[:, lane].astype(F32) * factor * gain_ref[j : j + 1, :].astype(F32)
        x_ref[:, lane] = scaled.astype(BF16)

    def step(i, _):
        rows_at = pl.ds(pl.multiple_of(i * depth, depth), depth)
        x = x_ref[:, rows_at]
        q_out[...] += jnp.dot(x, q_held[rows_at, :], preferred_element_type=F32)
        for j in range(kv_held.shape[0]):
            kv_out[j] += jnp.dot(x, kv_held[j, rows_at, :], preferred_element_type=F32)
        return 0

    lax.fori_loop(0, wide // depth, step, 0)


def base_projections(hidden, gain, q_weights, kv_weights):
    rows, wide = hidden.shape
    q_cols, kv_cols = q_weights.shape[1], kv_weights.shape[2]
    pair = kv_weights.shape[0]
    vmem = pl.BlockSpec(memory_space=pltpu.VMEM)
    return pl.pallas_call(
        base_kernel,
        in_specs=[vmem] * 4,
        out_specs=[vmem] * 3,
        out_shape=[
            jax.ShapeDtypeStruct((rows, wide), BF16),
            jax.ShapeDtypeStruct((rows, q_cols), F32),
            jax.ShapeDtypeStruct((pair, rows, kv_cols), F32),
        ],
        compiler_params=params(6),
        cost_estimate=pl.CostEstimate(
            flops=16 * rows * (q_weights.size + kv_weights.size),
            bytes_accessed=2 * (q_weights.size + kv_weights.size),
            transcendentals=0,
        ),
        name="base",
    )(gain.reshape(wide // 128, 128), hidden, q_weights, kv_weights)


def inner_kernel(x_ref, *refs):
    blocks, out_ref = refs[:-1], refs[-1]
    order = rep_order()
    tp, t = lax.axis_size("tp"), lax.axis_index("tp")
    ranks, deep = blocks[0].shape
    total = jnp.zeros((x_ref.shape[0], ranks), F32)
    for j, block in enumerate(blocks):
        at = pl.multiple_of((order[j] * tp + t) * deep, deep)
        total += lax.dot_general(
            x_ref[:, pl.ds(at, deep)],
            block[...],
            (((1,), (1,)), ((), ())),
            preferred_element_type=F32,
        )
    rest = jnp.zeros((x_ref.shape[0], out_ref.shape[1] - ranks), F32)
    out_ref[...] = jnp.concatenate([total, rest], axis=1).astype(BF16)


def partial_inner(normed, blocks):
    ranks, deep = blocks[0].shape
    rows = normed.shape[0]
    padded = -(-ranks // 128) * 128
    vmem = pl.BlockSpec(memory_space=pltpu.VMEM)
    if deep % 128 == 0:
        return pl.pallas_call(
            inner_kernel,
            in_specs=[vmem] * (1 + len(blocks)),
            out_specs=vmem,
            out_shape=jax.ShapeDtypeStruct((rows, padded), BF16),
            compiler_params=params(4),
            cost_estimate=pl.CostEstimate(flops=INNER, bytes_accessed=1 << 20, transcendentals=0),
            name="inner",
        )(normed, *blocks)
    total = jnp.zeros((rows, ranks), F32)
    tp, t = lax.axis_size("tp"), lax.axis_index("tp")
    for place, block in zip(rep_order(), blocks):
        place = place * tp + t
        own = lax.dynamic_slice_in_dim(normed, place * deep, deep, 1)
        total += jnp.dot(own, block.T, preferred_element_type=F32)
    return jnp.pad(total, ((0, 0), (0, padded - ranks))).astype(BF16)


def assemble_kernel(*refs, widths, count):
    blocks, outs = refs[:count], refs[count:]
    order = rep_order()
    offset = 0
    for width, out_ref in zip(widths, outs):
        total = out_ref.shape[1]
        if width % 128 == 0:
            for j, block in enumerate(blocks):
                at = pl.multiple_of(order[j] * width, 128)
                out_ref[:, pl.ds(at, width)] = block[:, offset : offset + width]
        else:
            placed = jnp.zeros((out_ref.shape[0], total), F32)
            source = lax.broadcasted_iota(jnp.int32, (width, total), 0)
            target = lax.broadcasted_iota(jnp.int32, (width, total), 1)
            for j, block in enumerate(blocks):
                chosen = (target == source + order[j] * width).astype(BF16)
                placed += jnp.dot(
                    block[:, offset : offset + width], chosen, preferred_element_type=F32
                )
            out_ref[...] = placed.astype(BF16)
        offset += width


def assemble(blocks, widths):
    rank = blocks[0].shape[0]
    count = len(blocks)
    vmem = pl.BlockSpec(memory_space=pltpu.VMEM)
    return pl.pallas_call(
        functools.partial(assemble_kernel, widths=widths, count=count),
        in_specs=[vmem] * count,
        out_specs=[vmem] * len(widths),
        out_shape=[jax.ShapeDtypeStruct((rank, w * count), BF16) for w in widths],
        compiler_params=params(4),
        name="assemble",
    )(*blocks)


def attend_kernel(
    lengths_ref, q_ref, kv_ref, q_up, k_up, v_up, od_ref, cos_ref, sin_ref, *refs,
    parts, group, block, far,
):
    parts_refs = refs[:parts]
    keys, values, weights, ctx_ref, pm_ref, out_ref = refs[parts : parts + 6]
    qs, nk, nv, cs = refs[parts + 6 :]
    rows, dim = cos_ref.shape
    heads = q_ref.shape[1] // dim
    kv = heads // group
    rank = q_up.shape[0]
    scale = 1.0 / math.sqrt(dim)
    count = rows // block
    wide = out_ref.shape[1] - pm_ref.shape[1]
    size = 512 if wide % 512 == 0 else wide
    column = exchange(lax.axis_size("tp"))(lax.axis_index("tp"), far) * wide

    total = parts_refs[0][...].astype(F32)
    for other in parts_refs[1:]:
        total += other[...].astype(F32)
    inner = total.astype(BF16)
    cosine, sine = cos_ref[...], sin_ref[...]

    def turned(x):
        return x * cosine + pltpu.roll(x, dim // 2, 1) * sine

    def delta(j, up):
        return adapter_scale * jnp.dot(
            inner[:, j * rank : (j + 1) * rank], up[...], preferred_element_type=F32
        )

    key_delta, value_delta, query_delta = delta(1, k_up), delta(2, v_up), delta(0, q_up)
    for g in range(kv):
        lane = slice(g * dim, (g + 1) * dim)
        key = turned(kv_ref[0, :, lane] + key_delta[:, lane]).astype(BF16).astype(F32)
        value = (kv_ref[1, :, lane] + value_delta[:, lane]).astype(BF16).astype(F32)
        for h in range(g * group, (g + 1) * group):
            lane = slice(h * dim, (h + 1) * dim)
            strided = pl.ds(h, rows, stride=heads)
            qs[strided, :] = turned(q_ref[:, lane] + query_delta[:, lane])
            nk[strided, :] = key
            nv[strided, :] = value

    row = lax.broadcasted_iota(jnp.int32, (heads, dim), 0)
    positions = keys.shape[2]
    spot = lax.broadcasted_iota(jnp.int32, (heads, positions), 1)

    def select(pieces):
        out = pieces[0]
        for g in range(1, kv):
            out = jnp.where(row >= g * group, pieces[g], out)
        return out

    def step(i, _):
        span = pl.ds(pl.multiple_of(i * block * heads, block * heads), block * heads)
        query = qs[span, :]
        high = query.astype(BF16)
        rest = query - high.astype(F32)
        mid = rest.astype(BF16)
        low = (rest - mid.astype(F32)).astype(BF16)
        found = []
        for b in range(block):
            s = i * block + b
            at = slice(b * heads, (b + 1) * heads)
            q = jnp.concatenate([high[at], mid[at], low[at]], axis=0)
            pieces = []
            for g in range(kv):
                full = lax.dot_general(
                    q, keys[s, g], (((1,), (1,)), ((), ())), preferred_element_type=F32
                )
                pieces.append(full[:heads] + (full[heads : 2 * heads] + full[2 * heads :]))
            found.append(jnp.where(spot < lengths_ref[s], select(pieces) * scale, -1e30))
        scores = jnp.concatenate(found, axis=0)
        own_score = jnp.sum(query * nk[span, :], axis=-1, keepdims=True) * scale
        top = jnp.maximum(jnp.max(scores, axis=-1, keepdims=True), own_score)
        exps = jnp.exp(scores - top)
        own_weight = jnp.exp(own_score - top)
        denom = jnp.sum(exps, axis=-1, keepdims=True) + own_weight
        inverse = 1.0 / denom
        probs = (exps * inverse).astype(BF16)
        own_prob = (own_weight * inverse).astype(BF16).astype(F32)
        found = []
        for b in range(block):
            s = i * block + b
            p = probs[b * heads : (b + 1) * heads]
            pieces = [
                jnp.dot(p, values[s, g], preferred_element_type=F32) for g in range(kv)
            ]
            found.append(select(pieces))
        cs[span, :] = jnp.concatenate(found, axis=0) + own_prob * nv[span, :]
        return 0

    lax.fori_loop(0, count, step, 0)

    middle = jnp.zeros((rows, rank), F32)
    for h in range(heads):
        lane = slice(h * dim, (h + 1) * dim)
        context = cs[pl.ds(h, rows, stride=heads), :].astype(BF16)
        ctx_ref[:, lane] = context
        middle += lax.dot_general(
            context, od_ref[:, lane], (((1,), (1,)), ((), ())), preferred_element_type=F32
        )
    high = middle.astype(BF16)
    low = (middle - high.astype(F32)).astype(BF16)
    tail = jnp.concatenate([high, low], axis=1)
    pm_ref[...] = tail

    def project(n, _):
        lane = pl.ds(pl.multiple_of(n * size, size), size)
        at = pl.ds(pl.multiple_of(column + n * size, size), size)
        part = jnp.dot(ctx_ref[...], weights[:, at], preferred_element_type=F32)
        out_ref[:, lane] = part.astype(BF16)
        return 0

    lax.fori_loop(0, wide // size, project, 0)
    out_ref[:, wide:] = tail


def attention(lengths, base_q, base_kv, parts, ups, od, angles, keys, values, weights, far):
    rows, kv, positions, dim = keys.shape
    q_cols = base_q.shape[1]
    heads = q_cols // dim
    rank = od.shape[0]
    block = 16 if rows % 16 == 0 else rows
    wide = weights.shape[1] // lax.axis_size("tp")
    vmem = pl.BlockSpec(memory_space=pltpu.VMEM)
    fixed = [base_q, base_kv] + list(ups) + [od] + list(angles) + list(parts)
    scratch = pltpu.VMEM((rows * heads, dim), F32)
    return pl.pallas_call(
        functools.partial(
            attend_kernel, parts=len(parts), group=heads // kv, block=block, far=far
        ),
        in_specs=[pl.BlockSpec(memory_space=pltpu.SMEM)] + [vmem] * (len(fixed) + 3),
        out_specs=[vmem, vmem, vmem],
        scratch_shapes=[
            scratch,
            scratch,
            scratch,
            scratch,
        ],
        out_shape=[
            jax.ShapeDtypeStruct((rows, q_cols), BF16),
            jax.ShapeDtypeStruct((rows, 2 * rank), BF16),
            jax.ShapeDtypeStruct((rows, wide + 2 * rank), BF16),
        ],
        compiler_params=params(8),
        cost_estimate=pl.CostEstimate(
            flops=4 * rows * heads * positions * dim * 16,
            bytes_accessed=4 * keys.size,
            transcendentals=rows * heads * positions,
        ),
        name="attend",
    )(lengths, *fixed, keys, values, weights)


def chunk_kernel(ctx_ref, w_ref, pm_ref, out_ref, *, k):
    wide = out_ref.shape[1] - (pm_ref.shape[1] if k else 0)
    size = 512 if wide % 512 == 0 else wide
    column = exchange(lax.axis_size("tp"))(lax.axis_index("tp"), k) * wide

    def project(n, _):
        lane = pl.ds(pl.multiple_of(n * size, size), size)
        at = pl.ds(pl.multiple_of(column + n * size, size), size)
        part = jnp.dot(ctx_ref[...], w_ref[:, at], preferred_element_type=F32)
        out_ref[:, lane] = part.astype(out_ref.dtype)
        return 0

    lax.fori_loop(0, wide // size, project, 0)
    if k:
        out_ref[:, wide:] = pm_ref[...]


def chunk(context, weights, middle, k):
    rows, depth = context.shape
    wide = weights.shape[1] // lax.axis_size("tp")
    tail = middle.shape[1] if k else 0
    vmem = pl.BlockSpec(memory_space=pltpu.VMEM)
    return pl.pallas_call(
        functools.partial(chunk_kernel, k=k),
        in_specs=[vmem, vmem, vmem],
        out_specs=vmem,
        out_shape=jax.ShapeDtypeStruct((rows, wide + tail), BF16 if k else F32),
        compiler_params=params(4),
        cost_estimate=pl.CostEstimate(
            flops=2 * rows * depth * wide, bytes_accessed=2 * depth * wide, transcendentals=0
        ),
    )(context, weights, middle)


def final_kernel(own_ref, pm_ref, up_ref, *refs):
    others, out_ref = refs[:-1], refs[-1]
    wide = own_ref.shape[1]
    rank = up_ref.shape[0]
    total = own_ref[...]
    middle = pm_ref[:, :rank].astype(F32) + pm_ref[:, rank:].astype(F32)
    for other in others:
        total += other[:, :wide].astype(F32)
        tail = other[:, wide:].astype(F32)
        middle += tail[:, :rank] + tail[:, rank:]
    total += adapter_scale * jnp.dot(
        middle.astype(BF16), up_ref[...], preferred_element_type=F32
    )
    out_ref[...] = total.astype(BF16)


def finish(own, middle, out_up, others):
    args = [own, middle, out_up] + others
    return pl.pallas_call(
        final_kernel,
        grid=(1,),
        in_specs=[whole(a.shape) for a in args],
        out_specs=whole(own.shape),
        out_shape=jax.ShapeDtypeStruct(own.shape, BF16),
        compiler_params=params(8),
        name="final",
    )(*args)


def local(
    hidden,
    norm_gain,
    query_weight_matrix,
    key_value_weight,
    output_weight_matrix,
    input_down_factors,
    query_up_factor,
    key_value_up_factors,
    output_down_factor,
    output_up_factor,
    cache_keys,
    cache_values,
    lengths,
):
    rep = lax.axis_size("rep")
    tp = lax.axis_size("tp")

    head_dim = cache_keys.shape[3]
    count, deep, rank = input_down_factors.shape
    input_down_factors, opened = lax.optimization_barrier((input_down_factors, opening()))
    cosine, sine = tables(lengths, opened, head_dim)
    down = input_down_factors.transpose(0, 2, 1).reshape(count * rank, deep)
    down_blocks = gather_rep(down)
    up_pack, widths = pack(
        query_up_factor, output_down_factor, output_up_factor, key_value_up_factors
    )
    moved = lax.ppermute(
        up_pack, ("rep", "tp"), [(b, (b % rep) * tp + b // rep) for b in range(rep * tp)]
    )
    normed, base_q, base_kv = base_projections(
        hidden, norm_gain, query_weight_matrix, key_value_weight
    )
    moved, base_q = lax.optimization_barrier((moved, base_q))
    up_blocks = gather_rep(moved)
    part = partial_inner(normed, down_blocks)
    parts = [part]
    for k in range(1, tp):
        parts.append(hop(part, "tp", k))
    q_up, od, out_up, k_up, v_up = assemble(up_blocks, widths)
    far = tp - 1
    context, middle, piece = attention(
        lengths, base_q, base_kv, parts, (q_up, k_up, v_up), od, (cosine, sine),
        cache_keys, cache_values, output_weight_matrix, far,
    )
    others = [hop(piece, "tp", far)]
    for k in range(far - 1, 0, -1):
        piece = chunk(context, output_weight_matrix, middle, k)
        others.append(hop(piece, "tp", k))
    own = chunk(context, output_weight_matrix, middle, 0)
    return finish(own, middle, out_up, others)


def solution(mesh):
    return jax.shard_map(
        local,
        mesh=mesh,
        in_specs=(
            P("rep", None),
            P(),
            P(None, "tp"),
            P(None, None, "tp"),
            P("tp", None),
            P(None, ("rep", "tp"), None),
            P(None, ("rep", "tp")),
            P(None, None, ("rep", "tp")),
            P(("rep", "tp"), None),
            P(None, ("rep", "tp")),
            P("rep", "tp", None, None),
            P("rep", "tp", None, None),
            P("rep"),
        ),
        out_specs=P("rep", "tp"),
        check_vma=False,
    )
```

time: 80.4 us -> 71.2 us (0.89)
  the two profiles are of different devices: /device:TPU:12 before, /device:TPU:15 now
where the time goes in v1:
time: 71.2 us; the launch traced here: 71 us
  waiting for transfers between devices  29.8 us (42%)
  starting transfers between devices  20.8 us (29%)
  Pallas kernels  19.3 us (27%)
  local copies, waits for them, and re-layouts  0.88 us (1%)
    ppermute x20, waiting for transfers between devices, hop(): return lax.ppermute(x, axis, [(i, to(i, k)) for i in range(n)])  29.8 us
    ppermute x20, starting transfers between devices, hop(): return lax.ppermute(x, axis, [(i, to(i, k)) for i in range(n)])  16.4 us
    pallas_call x1, Pallas kernels, base_projections(): pl.pallas_call(base_kernel, in_specs=[vmem] * 4, out_specs=[vmem] * 3, ou...  6.81 us
    pallas_call x1, Pallas kernels, attention(): pl.pallas_call(functools.partial(attend_kernel, parts=len(parts), group=h...  6.25 us
    ppermute x1, starting transfers between devices, local(): lax.ppermute(up_pack, ('rep', 'tp'), [(b, b % rep * tp + b // rep) for b...  4.45 us
    pallas_call x3, Pallas kernels, chunk(): pl.pallas_call(functools.partial(chunk_kernel, k=k), in_specs=[vmem, vmem...  3.65 us
  transfers between devices with their start and end apart: 21, of which 7 were waited for; matrix products, arithmetic and copies ran while one was open for 0% of the time, Pallas kernels for 13%

profile of v1, /device:TPU:15, one launch (start us, length us, event | category | flops | bytes accessed | tf_op | source)
XLA Modules:
  0.0 71.0 jit_solution(8868650377092607126)
XLA Ops:
  0.0 0.0 copy-start.5
  0.0 0.0 copy-start.3
  0.0 0.0 copy-start.8
  0.0 0.0 copy-start.7
  0.0 0.0 copy-start.11
  0.1 0.0 copy-start.9
  0.1 0.8 %copy-done.10 = bf16[3,256,64]{1,2,0:T(8,128)(2,1)S(1)} copy-done((bf16[3,256,64]{1,2,0:T(8,128)(2,1)S(1)}, bf16[3,256,64]{1,2,0:T(8,128)(2,1)}, u32[]{:S(2)}) %copy-start.10) | copy-done | bytes 98328
  0.9 0.7 collective-permute-start.11
  1.6 0.2 collective-permute-start.10
  1.8 1.2 %collective-permute-start.9 = (bf16[192,256]{1,0:T(8,128)(2,1)S(1)}, bf16[192,256]{1,0:T(8,128)(2,1)S(1)}, u32[]{:S(2)}, u32[]{:S(2)}) collective-permute-start(bf16[192,256]{1,0:T(8,128)(2,1)S(1)} %bitcast.12), channel_id=1, source_target_pairs={{0,16},{4,20},{8,24},{12,28},{16,0},{20,4},{24,8},{28,12},{1,17},{... | collective-permute-start | bytes 294920 | tf_op jit(solution)/shard_map/ppermute | solution.py:44
  3.0 1.2 %collective-permute-start.8 = (bf16[192,256]{1,0:T(8,128)(2,1)S(1)}, bf16[192,256]{1,0:T(8,128)(2,1)S(1)}, u32[]{:S(2)}, u32[]{:S(2)}) collective-permute-start(bf16[192,256]{1,0:T(8,128)(2,1)S(1)} %bitcast.13), channel_id=1, source_target_pairs={{0,8},{4,12},{8,0},{12,4},{16,24},{20,28},{24,16},{28,20},{1,9},{5... | collective-permute-start | bytes 294920 | tf_op jit(solution)/shard_map/ppermute | solution.py:44
  4.2 0.1 pack.1
  4.3 4.5 %collective-permute-start = (bf16[64,576]{1,0:T(8,128)(2,1)S(1)}, bf16[64,576]{1,0:T(8,128)(2,1)S(1)}, u32[]{:S(2)}, u32[]{:S(2)}) collective-permute-start(bf16[64,576]{1,0:T(8,128)(2,1)S(1)} %pack.1), channel_id=1, source_target_pairs={{0,0},{1,4},{2,8},{3,12},{4,16},{5,20},{6,24},{7,28},{8,1},{9,5},{... | collective-permute-start | bytes 221192 | tf_op jit(solution)/shard_map/ppermute | solution.py:523
  8.8 0.0 copy-done.7
  8.8 0.0 slice-start
  8.8 0.0 slice-start.1
  8.8 0.0 slice-start.2
  8.9 6.8 %base.1 = (bf16[64,8192]{1,0:T(8,128)(2,1)S(1)}, f32[64,1024]{1,0:T(8,128)S(1)}, f32[2,64,256]{2,1,0:T(8,128)S(1)}) custom-call(bf16[64,128]{1,0:T(8,128)(2,1)S(1)} %bitcast.15, bf16[64,8192]{1,0:T(8,128)(2,1)S(1)} %copy-done.9, bf16[8192,1024]{1,0:T(8,128)(2,1)S(1)} %copy-done.7, bf16[2,8192,256]{2,1,0:T(8,128)(2,1)S(1)} %copy-done.8), custom_call_target="tpu_custom_call" | custom-call | flops 12884901888 | bytes 25165824 | tf_op jit(solution)/shard_map/base/pallas_call | solution.py:180
  15.7 0.0 collective-permute-done.refs_0_
  15.7 0.1 collective-permute-start.3
  15.8 0.0 collective-permute-done.10.refs_3_
  15.8 0.8 %collective-permute-start.14 = (bf16[192,256]{1,0:T(8,128)(2,1)S(1)}, bf16[192,256]{1,0:T(8,128)(2,1)S(1)}, u32[]{:S(2)}, u32[]{:S(2)}) collective-permute-start(bf16[192,256]{1,0:T(8,128)(2,1)S(1)} %collective-permute-done.10.refs_3_), channel_id=1, source_target_pairs={{0,4},{4,0},{8,12},{12,8},{16,20},{20,16},{24,28},{28,24},{1,5},{5... | collective-permute-start | bytes 294920 | tf_op jit(solution)/shard_map/ppermute | solution.py:44
  16.6 0.0 collective-permute-done.9.refs_2_
  16.6 0.1 collective-permute-start.13
  16.7 0.0 collective-permute-done.8.refs_1_
  16.7 0.4 collective-permute-start.12
  17.1 0.0 collective-permute-done.11.refs_4_
  17.1 1.2 %collective-permute-start.2 = (bf16[64,576]{1,0:T(8,128)(2,1)S(1)}, bf16[64,576]{1,0:T(8,128)(2,1)S(1)}, u32[]{:S(2)}, u32[]{:S(2)}) collective-permute-start(bf16[64,576]{1,0:T(8,128)(2,1)S(1)} %collective-permute-done.refs_0_), channel_id=1, source_target_pairs={{0,16},{4,20},{8,24},{12,28},{16,0},{20,4},{24,8},{28,12},{1,17},{... | collective-permute-start | bytes 221192 | tf_op jit(solution)/shard_map/ppermute | solution.py:44
  18.3 2.0 %collective-permute-done.3.refs_3_ = bf16[64,576]{1,0:T(8,128)(2,1)S(1)} collective-permute-done((bf16[64,576]{1,0:T(8,128)(2,1)S(1)}, bf16[64,576]{1,0:T(8,128)(2,1)S(1)}, u32[]{:S(2)}, u32[]{:S(2)}) %collective-permute-start.3) | collective-permute-done | bytes 73760 | tf_op jit(solution)/shard_map/ppermute | solution.py:44
  20.3 0.0 collective-permute-start.1
  20.3 2.5 %collective-permute-done.2.refs_2_ = bf16[64,576]{1,0:T(8,128)(2,1)S(1)} collective-permute-done((bf16[64,576]{1,0:T(8,128)(2,1)S(1)}, bf16[64,576]{1,0:T(8,128)(2,1)S(1)}, u32[]{:S(2)}, u32[]{:S(2)}) %collective-permute-start.2) | collective-permute-done | bytes 73760 | tf_op jit(solution)/shard_map/ppermute | solution.py:44
  22.8 0.4 collective-permute-start.4
  23.3 0.3 collective-permute-done.1.refs_1_
  23.6 2.5 %collective-permute-start.7 = (bf16[64,576]{1,0:T(8,128)(2,1)S(1)}, bf16[64,576]{1,0:T(8,128)(2,1)S(1)}, u32[]{:S(2)}, u32[]{:S(2)}) collective-permute-start(bf16[64,576]{1,0:T(8,128)(2,1)S(1)} %collective-permute-done.3.refs_3_), channel_id=1, source_target_pairs={{0,4},{4,0},{8,12},{12,8},{16,20},{20,16},{24,28},{28,24},{1,5},{5... | collective-permute-start | bytes 221192 | tf_op jit(solution)/shard_map/ppermute | solution.py:44
  26.0 0.0 collective-permute-done.14.refs_7_
  26.0 0.0 collective-permute-start.6
  26.1 0.0 collective-permute-done.13.refs_6_
  26.1 0.5 collective-permute-start.5
  26.6 0.0 collective-permute-done.12.refs_5_
  26.6 0.0 copy-start.1
  26.6 0.4 inner.1.refs_0_
  27.0 1.2 %collective-permute-start.17 = (bf16[64,256]{1,0:T(8,128)(2,1)S(1)}, bf16[64,256]{1,0:T(8,128)(2,1)S(1)}, u32[]{:S(2)}, u32[]{:S(2)}) collective-permute-start(bf16[64,256]{1,0:T(8,128)(2,1)S(1)} %inner.1.refs_0_), channel_id=1, source_target_pairs={{0,3},{1,2},{2,1},{3,0},{4,7},{5,6},{6,5},{7,4},{8,11},{9,10},{10,... | collective-permute-start | bytes 98312 | tf_op jit(solution)/shard_map/ppermute | solution.py:44
  28.2 0.0 collective-permute-done.4.refs_4_
  28.2 2.9 %collective-permute-start.16 = (bf16[64,256]{1,0:T(8,128)(2,1)S(1)}, bf16[64,256]{1,0:T(8,128)(2,1)S(1)}, u32[]{:S(2)}, u32[]{:S(2)}) collective-permute-start(bf16[64,256]{1,0:T(8,128)(2,1)S(1)} %inner.1.refs_0_), channel_id=1, source_target_pairs={{0,2},{1,3},{2,0},{3,1},{4,6},{5,7},{6,4},{7,5},{8,10},{9,11},{10,... | collective-permute-start | bytes 98312 | tf_op jit(solution)/shard_map/ppermute | solution.py:44
  31.0 0.0 collective-permute-done.7.refs_7_
  31.0 0.0 collective-permute-start.15
  31.0 0.8 %tables.1 = (f32[64,128]{1,0:T(8,128)S(1)}, f32[64,128]{1,0:T(8,128)S(1)}) custom-call(s32[64]{0:T(128)S(1)} %copy-done.6, f32[8,128]{1,0:T(8,128)S(1)} %opening.1._), custom_call_target="tpu_custom_call" | custom-call | tf_op jit(solution)/shard_map/tables/pallas_call | solution.py:135
  31.8 0.0 collective-permute-done.6.refs_6_
  31.8 0.0 collective-permute-done.5.refs_5_
  31.8 0.3 assemble.1
  32.2 0.0 collective-permute-done.17.refs_3_
  32.2 0.7 collective-permute-done.16.refs_2_
  32.9 0.9 %collective-permute-done.15.refs_1_ = bf16[64,256]{1,0:T(8,128)(2,1)S(1)} collective-permute-done((bf16[64,256]{1,0:T(8,128)(2,1)S(1)}, bf16[64,256]{1,0:T(8,128)(2,1)S(1)}, u32[]{:S(2)}, u32[]{:S(2)}) %collective-permute-start.15) | collective-permute-done | bytes 32800 | tf_op jit(solution)/shard_map/ppermute | solution.py:44
  33.8 6.3 %attend.1 = (bf16[64,1024]{1,0:T(8,128)(2,1)S(1)}, bf16[64,128]{1,0:T(8,128)(2,1)S(1)}, bf16[64,2176]{1,0:T(8,128)(2,1)S(1)}) custom-call(s32[64]{0:T(128)S(1)} %copy-done.6, f32[64,1024]{1,0:T(8,128)S(1)} %get-tuple-element.23.q_ref, f32[2,64,256]{2,1,0:T(8,128)S(1)} %get-tuple-element.24.kv_ref, bf16[64,1024]{1,0:T(8,128)(2,1)S(1)} %get-tuple-element.26.q_up, ...), custom_call_target="tpu_custom_call" | custom-call | flops 536870912 | bytes 8388608 | tf_op jit(solution)/shard_map/attend/pallas_call | solution.py:406
  40.1 1.2 %shard_map.129 = bf16[64,2176]{1,0:T(8,128)(2,1)S(1)} custom-call(bf16[64,1024]{1,0:T(8,128)(2,1)S(1)} %get-tuple-element.35.ctx_ref, bf16[1024,8192]{1,0:T(8,128)(2,1)S(1)} %bitcast.7, bf16[64,128]{1,0:T(8,128)(2,1)S(1)} %get-tuple-element.36.pm_ref), custom_call_target="tpu_custom_call" | custom-call | flops 268435456 | bytes 4194304 | tf_op jit(solution)/shard_map/pallas_call | solution.py:455
  41.3 1.2 %shard_map.128 = bf16[64,2176]{1,0:T(8,128)(2,1)S(1)} custom-call(bf16[64,1024]{1,0:T(8,128)(2,1)S(1)} %get-tuple-element.35.ctx_ref, bf16[1024,8192]{1,0:T(8,128)(2,1)S(1)} %bitcast.7, bf16[64,128]{1,0:T(8,128)(2,1)S(1)} %get-tuple-element.36.pm_ref), custom_call_target="tpu_custom_call" | custom-call | flops 268435456 | bytes 4194304 | tf_op jit(solution)/shard_map/pallas_call | solution.py:455
  42.6 1.4 %collective-permute-start.19 = (bf16[64,2176]{1,0:T(8,128)(2,1)S(1)}, bf16[64,2176]{1,0:T(8,128)(2,1)S(1)}, u32[]{:S(2)}, u32[]{:S(2)}) collective-permute-start(bf16[64,2176]{1,0:T(8,128)(2,1)S(1)} %shard_map.128), channel_id=1, source_target_pairs={{0,2},{1,3},{2,0},{3,1},{4,6},{5,7},{6,4},{7,5},{8,10},{9,11},{10,... | collective-permute-start | bytes 835592 | tf_op jit(solution)/shard_map/ppermute | solution.py:44
  44.0 0.4 collective-permute-start.20
  44.4 1.1 %collective-permute-start.18 = (bf16[64,2176]{1,0:T(8,128)(2,1)S(1)}, bf16[64,2176]{1,0:T(8,128)(2,1)S(1)}, u32[]{:S(2)}, u32[]{:S(2)}) collective-permute-start(bf16[64,2176]{1,0:T(8,128)(2,1)S(1)} %get-tuple-element.38), channel_id=1, source_target_pairs={{0,3},{1,2},{2,1},{3,0},{4,7},{5,6},{6,5},{7,4},{8,11},{9,10},{10,... | collective-permute-start | bytes 835592 | tf_op jit(solution)/shard_map/ppermute | solution.py:44
  45.5 1.2 %shard_map.127.own_ref = f32[64,2048]{1,0:T(8,128)S(1)} custom-call(bf16[64,1024]{1,0:T(8,128)(2,1)S(1)} %get-tuple-element.35.ctx_ref, bf16[1024,8192]{1,0:T(8,128)(2,1)S(1)} %bitcast.7, bf16[64,128]{1,0:T(8,128)(2,1)S(1)} %get-tuple-element.36.pm_ref), custom_call_target="tpu_custom_call" | custom-call | flops 268435456 | bytes 4194304 | tf_op jit(solution)/shard_map/pallas_call | solution.py:455
  46.7 11.1 %collective-permute-done.19.refs_1_ = bf16[64,2176]{1,0:T(8,128)(2,1)S(1)} collective-permute-done((bf16[64,2176]{1,0:T(8,128)(2,1)S(1)}, bf16[64,2176]{1,0:T(8,128)(2,1)S(1)}, u32[]{:S(2)}, u32[]{:S(2)}) %collective-permute-start.19) | collective-permute-done | bytes 278560 | tf_op jit(solution)/shard_map/ppermute | solution.py:44
  57.8 0.0 collective-permute-done.20.refs_2_
  57.8 12.2 %collective-permute-done.18.refs_0_ = bf16[64,2176]{1,0:T(8,128)(2,1)S(1)} collective-permute-done((bf16[64,2176]{1,0:T(8,128)(2,1)S(1)}, bf16[64,2176]{1,0:T(8,128)(2,1)S(1)}, u32[]{:S(2)}, u32[]{:S(2)}) %collective-permute-start.18) | collective-permute-done | bytes 278560 | tf_op jit(solution)/shard_map/ppermute | solution.py:44
  70.0 1.0 %final.1 = bf16[64,2048]{1,0:T(8,128)(2,1)} custom-call(f32[64,2048]{1,0:T(8,128)S(1)} %shard_map.127.own_ref, bf16[64,128]{1,0:T(8,128)(2,1)S(1)} %get-tuple-element.36.pm_ref, bf16[64,2048]{1,0:T(8,128)(2,1)S(1)} %get-tuple-element.37.up_ref, bf16[64,2176]{1,0:T(8,128)(2,1)S(1)} %collective-permute-done.18.refs_0_, ...), custom_call_target="tpu_custom_call" | custom-call | tf_op jit(solution)/shard_map/final/pallas_call | solution.py:485
  (22 shorter events, 0.0 us)
Async XLA Ops:
  0.0 0.9 %copy-start.10 = (bf16[3,256,64]{1,2,0:T(8,128)(2,1)S(1)}, bf16[3,256,64]{1,2,0:T(8,128)(2,1)}, u32[]{:S(2)}) copy-start(bf16[3,256,64]{1,2,0:T(8,128)(2,1)} %param.18) | copy-start | bytes 294916
  0.0 4.2 %copy-start.2 = (bf16[64,256]{1,0:T(8,128)(2,1)S(1)}, bf16[64,256]{1,0:T(8,128)(2,1)}, u32[]{:S(2)}) copy-start(bf16[64,256]{1,0:T(8,128)(2,1)} %ou_ref.1) | copy-start | bytes 98308
  0.0 4.2 %copy-start.4 = (bf16[128,64]{0,1:T(8,128)(2,1)S(1)}, bf16[128,64]{0,1:T(8,128)(2,1)}, u32[]{:S(2)}) copy-start(bf16[128,64]{0,1:T(8,128)(2,1)} %param.21) | copy-start | bytes 49156
  0.0 4.2 %copy-start.5 = (bf16[2,64,32]{1,2,0:T(8,128)(2,1)S(1)}, bf16[2,64,32]{1,2,0:T(8,128)(2,1)}, u32[]{:S(2)}) copy-start(bf16[2,64,32]{1,2,0:T(8,128)(2,1)} %param.20) | copy-start | bytes 24580
  0.0 4.2 %copy-start.3 = (bf16[64,128]{1,0:T(8,128)(2,1)S(1)}, bf16[64,128]{1,0:T(8,128)(2,1)}, u32[]{:S(2)}) copy-start(bf16[64,128]{1,0:T(8,128)(2,1)} %q_ref.1) | copy-start | bytes 49156
  0.0 8.8 %copy-start.8 = (bf16[2,8192,256]{2,1,0:T(8,128)(2,1)S(1)}, bf16[2,8192,256]{2,1,0:T(8,128)(2,1)}, u32[]{:S(2)}) copy-start(bf16[2,8192,256]{2,1,0:T(8,128)(2,1)} %kv_held.1) | copy-start | bytes 25165828
  0.0 8.8 %copy-start.7 = (bf16[8192,1024]{1,0:T(8,128)(2,1)S(1)}, bf16[8192,1024]{1,0:T(8,128)(2,1)}, u32[]{:S(2)}) copy-start(bf16[8192,1024]{1,0:T(8,128)(2,1)} %q_held.1) | copy-start | bytes 50331652
  0.0 8.8 %copy-start.11 = (bf16[8192]{0:T(1024)(128)(2,1)S(1)}, bf16[8192]{0:T(1024)(128)(2,1)}, u32[]{:S(2)}) copy-start(bf16[8192]{0:T(1024)(128)(2,1)} %param.14) | copy-start | bytes 49156
  0.1 8.8 %copy-start.9 = (bf16[64,8192]{1,0:T(8,128)(2,1)S(1)}, bf16[64,8192]{1,0:T(8,128)(2,1)}, u32[]{:S(2)}) copy-start(bf16[64,8192]{1,0:T(8,128)(2,1)} %hidden.1) | copy-start | bytes 3145732
  0.9 16.2 %collective-permute-start.11 = (bf16[192,256]{1,0:T(8,128)(2,1)S(1)}, bf16[192,256]{1,0:T(8,128)(2,1)S(1)}, u32[]{:S(2)}, u32[]{:S(2)}) collective-permute-start(bf16[192,256]{1,0:T(8,128)(2,1)S(1)} %bitcast.10), channel_id=1, source_target_pairs={{0,4},{4,0},{8,12},{12,8},{16,20},{20,16},{24,28},{28,24},{1,5},{5... | collective-permute-start | bytes 294920 | tf_op jit(solution)/shard_map/ppermute | solution.py:44
  1.6 14.2 %collective-permute-start.10 = (bf16[192,256]{1,0:T(8,128)(2,1)S(1)}, bf16[192,256]{1,0:T(8,128)(2,1)S(1)}, u32[]{:S(2)}, u32[]{:S(2)}) collective-permute-start(bf16[192,256]{1,0:T(8,128)(2,1)S(1)} %bitcast.11), channel_id=1, source_target_pairs={{0,24},{4,28},{8,16},{12,20},{16,8},{20,12},{24,0},{28,4},{1,25},{... | collective-permute-start | bytes 294920 | tf_op jit(solution)/shard_map/ppermute | solution.py:44
  1.8 14.8 %collective-permute-start.9 = (bf16[192,256]{1,0:T(8,128)(2,1)S(1)}, bf16[192,256]{1,0:T(8,128)(2,1)S(1)}, u32[]{:S(2)}, u32[]{:S(2)}) collective-permute-start(bf16[192,256]{1,0:T(8,128)(2,1)S(1)} %bitcast.12), channel_id=1, source_target_pairs={{0,16},{4,20},{8,24},{12,28},{16,0},{20,4},{24,8},{28,12},{1,17},{... | collective-permute-start | bytes 294920 | tf_op jit(solution)/shard_map/ppermute | solution.py:44
  3.0 13.7 %collective-permute-start.8 = (bf16[192,256]{1,0:T(8,128)(2,1)S(1)}, bf16[192,256]{1,0:T(8,128)(2,1)S(1)}, u32[]{:S(2)}, u32[]{:S(2)}) collective-permute-start(bf16[192,256]{1,0:T(8,128)(2,1)S(1)} %bitcast.13), channel_id=1, source_target_pairs={{0,8},{4,12},{8,0},{12,4},{16,24},{20,28},{24,16},{28,20},{1,9},{5... | collective-permute-start | bytes 294920 | tf_op jit(solution)/shard_map/ppermute | solution.py:44
  4.3 11.4 %collective-permute-start = (bf16[64,576]{1,0:T(8,128)(2,1)S(1)}, bf16[64,576]{1,0:T(8,128)(2,1)S(1)}, u32[]{:S(2)}, u32[]{:S(2)}) collective-permute-start(bf16[64,576]{1,0:T(8,128)(2,1)S(1)} %pack.1), channel_id=1, source_target_pairs={{0,0},{1,4},{2,8},{3,12},{4,16},{5,20},{6,24},{7,28},{8,1},{9,5},{... | collective-permute-start | bytes 221192 | tf_op jit(solution)/shard_map/ppermute | solution.py:523
  8.8 25.0 %slice-start = ((s8[16777216]{0:T(1024)(128)(4,1)}), s8[4194304]{0:T(1024)(128)(4,1)S(1)}, s32[]{:S(2)}) async-start(s8[16777216]{0:T(1024)(128)(4,1)} %bitcast.6), calls=%async_computation | async-start | bytes 8388608
  8.8 25.0 %slice-start.1 = ((s8[16777216]{0:T(1024)(128)(4,1)}), s8[4194304]{0:T(1024)(128)(4,1)S(1)}, s32[]{:S(2)}) async-start(s8[16777216]{0:T(1024)(128)(4,1)} %bitcast.6), calls=%async_computation.1 | async-start | bytes 8388608
  8.8 25.0 %slice-start.2 = ((s8[16777216]{0:T(1024)(128)(4,1)}), s8[4194304]{0:T(1024)(128)(4,1)S(1)}, s32[]{:S(2)}) async-start(s8[16777216]{0:T(1024)(128)(4,1)} %bitcast.6), calls=%async_computation.2 | async-start | bytes 8388608
  15.7 4.6 %collective-permute-start.3 = (bf16[64,576]{1,0:T(8,128)(2,1)S(1)}, bf16[64,576]{1,0:T(8,128)(2,1)S(1)}, u32[]{:S(2)}, u32[]{:S(2)}) collective-permute-start(bf16[64,576]{1,0:T(8,128)(2,1)S(1)} %collective-permute-done.refs_0_), channel_id=1, source_target_pairs={{0,24},{4,28},{8,16},{12,20},{16,8},{20,12},{24,0},{28,4},{1,25},{... | collective-permute-start | bytes 221192 | tf_op jit(solution)/shard_map/ppermute | solution.py:44
  15.8 10.3 %collective-permute-start.14 = (bf16[192,256]{1,0:T(8,128)(2,1)S(1)}, bf16[192,256]{1,0:T(8,128)(2,1)S(1)}, u32[]{:S(2)}, u32[]{:S(2)}) collective-permute-start(bf16[192,256]{1,0:T(8,128)(2,1)S(1)} %collective-permute-done.10.refs_3_), channel_id=1, source_target_pairs={{0,4},{4,0},{8,12},{12,8},{16,20},{20,16},{24,28},{28,24},{1,5},{5... | collective-permute-start | bytes 294920 | tf_op jit(solution)/shard_map/ppermute | solution.py:44
  16.6 9.5 %collective-permute-start.13 = (bf16[192,256]{1,0:T(8,128)(2,1)S(1)}, bf16[192,256]{1,0:T(8,128)(2,1)S(1)}, u32[]{:S(2)}, u32[]{:S(2)}) collective-permute-start(bf16[192,256]{1,0:T(8,128)(2,1)S(1)} %collective-permute-done.9.refs_2_), channel_id=1, source_target_pairs={{0,4},{4,0},{8,12},{12,8},{16,20},{20,16},{24,28},{28,24},{1,5},{5... | collective-permute-start | bytes 294920 | tf_op jit(solution)/shard_map/ppermute | solution.py:44
  16.7 9.9 %collective-permute-start.12 = (bf16[192,256]{1,0:T(8,128)(2,1)S(1)}, bf16[192,256]{1,0:T(8,128)(2,1)S(1)}, u32[]{:S(2)}, u32[]{:S(2)}) collective-permute-start(bf16[192,256]{1,0:T(8,128)(2,1)S(1)} %collective-permute-done.8.refs_1_), channel_id=1, source_target_pairs={{0,4},{4,0},{8,12},{12,8},{16,20},{20,16},{24,28},{28,24},{1,5},{5... | collective-permute-start | bytes 294920 | tf_op jit(solution)/shard_map/ppermute | solution.py:44
  17.1 5.7 %collective-permute-start.2 = (bf16[64,576]{1,0:T(8,128)(2,1)S(1)}, bf16[64,576]{1,0:T(8,128)(2,1)S(1)}, u32[]{:S(2)}, u32[]{:S(2)}) collective-permute-start(bf16[64,576]{1,0:T(8,128)(2,1)S(1)} %collective-permute-done.refs_0_), channel_id=1, source_target_pairs={{0,16},{4,20},{8,24},{12,28},{16,0},{20,4},{24,8},{28,12},{1,17},{... | collective-permute-start | bytes 221192 | tf_op jit(solution)/shard_map/ppermute | solution.py:44
  20.3 3.3 %collective-permute-start.1 = (bf16[64,576]{1,0:T(8,128)(2,1)S(1)}, bf16[64,576]{1,0:T(8,128)(2,1)S(1)}, u32[]{:S(2)}, u32[]{:S(2)}) collective-permute-start(bf16[64,576]{1,0:T(8,128)(2,1)S(1)} %collective-permute-done.refs_0_), channel_id=1, source_target_pairs={{0,8},{4,12},{8,0},{12,4},{16,24},{20,28},{24,16},{28,20},{1,9},{5... | collective-permute-start | bytes 221192 | tf_op jit(solution)/shard_map/ppermute | solution.py:44
  22.8 5.4 %collective-permute-start.4 = (bf16[64,576]{1,0:T(8,128)(2,1)S(1)}, bf16[64,576]{1,0:T(8,128)(2,1)S(1)}, u32[]{:S(2)}, u32[]{:S(2)}) collective-permute-start(bf16[64,576]{1,0:T(8,128)(2,1)S(1)} %collective-permute-done.refs_0_), channel_id=1, source_target_pairs={{0,4},{4,0},{8,12},{12,8},{16,20},{20,16},{24,28},{28,24},{1,5},{5... | collective-permute-start | bytes 221192 | tf_op jit(solution)/shard_map/ppermute | solution.py:44
  23.6 7.4 %collective-permute-start.7 = (bf16[64,576]{1,0:T(8,128)(2,1)S(1)}, bf16[64,576]{1,0:T(8,128)(2,1)S(1)}, u32[]{:S(2)}, u32[]{:S(2)}) collective-permute-start(bf16[64,576]{1,0:T(8,128)(2,1)S(1)} %collective-permute-done.3.refs_3_), channel_id=1, source_target_pairs={{0,4},{4,0},{8,12},{12,8},{16,20},{20,16},{24,28},{28,24},{1,5},{5... | collective-permute-start | bytes 221192 | tf_op jit(solution)/shard_map/ppermute | solution.py:44
  26.0 5.8 %collective-permute-start.6 = (bf16[64,576]{1,0:T(8,128)(2,1)S(1)}, bf16[64,576]{1,0:T(8,128)(2,1)S(1)}, u32[]{:S(2)}, u32[]{:S(2)}) collective-permute-start(bf16[64,576]{1,0:T(8,128)(2,1)S(1)} %collective-permute-done.2.refs_2_), channel_id=1, source_target_pairs={{0,4},{4,0},{8,12},{12,8},{16,20},{20,16},{24,28},{28,24},{1,5},{5... | collective-permute-start | bytes 221192 | tf_op jit(solution)/shard_map/ppermute | solution.py:44
  26.1 5.8 %collective-permute-start.5 = (bf16[64,576]{1,0:T(8,128)(2,1)S(1)}, bf16[64,576]{1,0:T(8,128)(2,1)S(1)}, u32[]{:S(2)}, u32[]{:S(2)}) collective-permute-start(bf16[64,576]{1,0:T(8,128)(2,1)S(1)} %collective-permute-done.1.refs_1_), channel_id=1, source_target_pairs={{0,4},{4,0},{8,12},{12,8},{16,20},{20,16},{24,28},{28,24},{1,5},{5... | collective-permute-start | bytes 221192 | tf_op jit(solution)/shard_map/ppermute | solution.py:44
  26.6 4.5 %copy-start.6 = (s32[64]{0:T(128)S(1)}, s32[64]{0:T(128)}, u32[]{:S(2)}) copy-start(s32[64]{0:T(128)} %lengths_ref.3) | copy-start | bytes 772
  26.6 7.2 %slice-start.3 = ((s8[16777216]{0:T(1024)(128)(4,1)}), s8[4194304]{0:T(1024)(128)(4,1)S(1)}, s32[]{:S(2)}) async-start(s8[16777216]{0:T(1024)(128)(4,1)} %bitcast.6), calls=%async_computation.3 | async-start | bytes 8388608
  26.6 7.2 %copy-start = (bf16[64,2,128,128]{3,2,1,0:T(8,128)(2,1)S(1)}, bf16[64,2,128,128]{3,2,1,0:T(8,128)(2,1)}, u32[]{:S(2)}) copy-start(bf16[64,2,128,128]{3,2,1,0:T(8,128)(2,1)} %refs_4_.1) | copy-start | bytes 12582916
  26.6 7.3 %copy-start.1 = (bf16[64,2,128,128]{3,2,1,0:T(8,128)(2,1)S(1)}, bf16[64,2,128,128]{3,2,1,0:T(8,128)(2,1)}, u32[]{:S(2)}) copy-start(bf16[64,2,128,128]{3,2,1,0:T(8,128)(2,1)} %refs_5_.1) | copy-start | bytes 12582916
  27.0 5.2 %collective-permute-start.17 = (bf16[64,256]{1,0:T(8,128)(2,1)S(1)}, bf16[64,256]{1,0:T(8,128)(2,1)S(1)}, u32[]{:S(2)}, u32[]{:S(2)}) collective-permute-start(bf16[64,256]{1,0:T(8,128)(2,1)S(1)} %inner.1.refs_0_), channel_id=1, source_target_pairs={{0,3},{1,2},{2,1},{3,0},{4,7},{5,6},{6,5},{7,4},{8,11},{9,10},{10,... | collective-permute-start | bytes 98312 | tf_op jit(solution)/shard_map/ppermute | solution.py:44
  28.2 4.7 %collective-permute-start.16 = (bf16[64,256]{1,0:T(8,128)(2,1)S(1)}, bf16[64,256]{1,0:T(8,128)(2,1)S(1)}, u32[]{:S(2)}, u32[]{:S(2)}) collective-permute-start(bf16[64,256]{1,0:T(8,128)(2,1)S(1)} %inner.1.refs_0_), channel_id=1, source_target_pairs={{0,2},{1,3},{2,0},{3,1},{4,6},{5,7},{6,4},{7,5},{8,10},{9,11},{10,... | collective-permute-start | bytes 98312 | tf_op jit(solution)/shard_map/ppermute | solution.py:44
  31.0 2.8 %collective-permute-start.15 = (bf16[64,256]{1,0:T(8,128)(2,1)S(1)}, bf16[64,256]{1,0:T(8,128)(2,1)S(1)}, u32[]{:S(2)}, u32[]{:S(2)}) collective-permute-start(bf16[64,256]{1,0:T(8,128)(2,1)S(1)} %inner.1.refs_0_), channel_id=1, source_target_pairs={{0,1},{1,0},{2,3},{3,2},{4,5},{5,4},{6,7},{7,6},{8,9},{9,8},{10,11... | collective-permute-start | bytes 98312 | tf_op jit(solution)/shard_map/ppermute | solution.py:44
  42.6 15.3 %collective-permute-start.19 = (bf16[64,2176]{1,0:T(8,128)(2,1)S(1)}, bf16[64,2176]{1,0:T(8,128)(2,1)S(1)}, u32[]{:S(2)}, u32[]{:S(2)}) collective-permute-start(bf16[64,2176]{1,0:T(8,128)(2,1)S(1)} %shard_map.128), channel_id=1, source_target_pairs={{0,2},{1,3},{2,0},{3,1},{4,6},{5,7},{6,4},{7,5},{8,10},{9,11},{10,... | collective-permute-start | bytes 835592 | tf_op jit(solution)/shard_map/ppermute | solution.py:44
  44.0 13.8 %collective-permute-start.20 = (bf16[64,2176]{1,0:T(8,128)(2,1)S(1)}, bf16[64,2176]{1,0:T(8,128)(2,1)S(1)}, u32[]{:S(2)}, u32[]{:S(2)}) collective-permute-start(bf16[64,2176]{1,0:T(8,128)(2,1)S(1)} %shard_map.129), channel_id=1, source_target_pairs={{0,1},{1,0},{2,3},{3,2},{4,5},{5,4},{6,7},{7,6},{8,9},{9,8},{10,11... | collective-permute-start | bytes 835592 | tf_op jit(solution)/shard_map/ppermute | solution.py:44
  44.4 25.6 %collective-permute-start.18 = (bf16[64,2176]{1,0:T(8,128)(2,1)S(1)}, bf16[64,2176]{1,0:T(8,128)(2,1)S(1)}, u32[]{:S(2)}, u32[]{:S(2)}) collective-permute-start(bf16[64,2176]{1,0:T(8,128)(2,1)S(1)} %get-tuple-element.38), channel_id=1, source_target_pairs={{0,3},{1,2},{2,1},{3,0},{4,7},{5,6},{6,5},{7,4},{8,11},{9,10},{10,... | collective-permute-start | bytes 835592 | tf_op jit(solution)/shard_map/ppermute | solution.py:44

commit v2 on v1

--- a/solution.py
+++ b/solution.py
@@ -17,6 +17,7 @@
 
 
 INNER = 6 * 10**9
+LINE = ((3, 2, 1, 0), (2, 0, 3, 1), (1, 3, 0, 2))
 LONG = pl.CostEstimate(flops=1 << 34, bytes_accessed=1 << 20, transcendentals=0)
 
 
@@ -48,6 +49,16 @@
     if power_of_two(n):
         return index ^ k
     return (index - k) % n
+
+
+def chunk_target(target):
+    t = lax.axis_index("tp")
+    if isinstance(target, tuple):
+        found = target[0]
+        for place in range(1, len(target)):
+            found = jnp.where(t == place, target[place], found)
+        return found
+    return exchange(lax.axis_size("tp"))(t, target)
 
 
 def gather_rep(block):
@@ -290,7 +301,7 @@
     count = rows // block
     wide = out_ref.shape[1] - pm_ref.shape[1]
     size = 512 if wide % 512 == 0 else wide
-    column = exchange(lax.axis_size("tp"))(lax.axis_index("tp"), far) * wide
+    column = chunk_target(far) * wide
 
     total = parts_refs[0][...].astype(F32)
     for other in parts_refs[1:]:
@@ -328,8 +339,8 @@
             out = jnp.where(row >= g * group, pieces[g], out)
         return out
 
-    def step(i, _):
-        span = pl.ds(pl.multiple_of(i * block * heads, block * heads), block * heads)
+    def score(i):
+        span = slice(i * block * heads, (i + 1) * block * heads)
         query = qs[span, :]
         high = query.astype(BF16)
         rest = query - high.astype(F32)
@@ -347,15 +358,18 @@
                 )
                 pieces.append(full[:heads] + (full[heads : 2 * heads] + full[2 * heads :]))
             found.append(jnp.where(spot < lengths_ref[s], select(pieces) * scale, -1e30))
-        scores = jnp.concatenate(found, axis=0)
         own_score = jnp.sum(query * nk[span, :], axis=-1, keepdims=True) * scale
+        return jnp.concatenate(found, axis=0), own_score
+
+    def weigh(scores, own_score):
         top = jnp.maximum(jnp.max(scores, axis=-1, keepdims=True), own_score)
         exps = jnp.exp(scores - top)
         own_weight = jnp.exp(own_score - top)
-        denom = jnp.sum(exps, axis=-1, keepdims=True) + own_weight
-        inverse = 1.0 / denom
-        probs = (exps * inverse).astype(BF16)
-        own_prob = (own_weight * inverse).astype(BF16).astype(F32)
+        inverse = 1.0 / (jnp.sum(exps, axis=-1, keepdims=True) + own_weight)
+        return (exps * inverse).astype(BF16), (own_weight * inverse).astype(BF16).astype(F32)
+
+    def gather(i, probs, own_prob):
+        span = slice(i * block * heads, (i + 1) * block * heads)
         found = []
         for b in range(block):
             s = i * block + b
@@ -365,9 +379,15 @@
             ]
             found.append(select(pieces))
         cs[span, :] = jnp.concatenate(found, axis=0) + own_prob * nv[span, :]
-        return 0
-
-    lax.fori_loop(0, count, step, 0)
+
+    scored, weighed = None, None
+    for i in range(count + 2):
+        if i >= 2:
+            gather(i - 2, *weighed)
+        if 1 <= i <= count:
+            weighed = weigh(*scored)
+        if i < count:
+            scored = score(i)
 
     middle = jnp.zeros((rows, rank), F32)
     for h in range(heads):
@@ -433,7 +453,7 @@
 def chunk_kernel(ctx_ref, w_ref, pm_ref, out_ref, *, k):
     wide = out_ref.shape[1] - (pm_ref.shape[1] if k else 0)
     size = 512 if wide % 512 == 0 else wide
-    column = exchange(lax.axis_size("tp"))(lax.axis_index("tp"), k) * wide
+    column = chunk_target(k) * wide
 
     def project(n, _):
         lane = pl.ds(pl.multiple_of(n * size, size), size)
@@ -462,6 +482,29 @@
             flops=2 * rows * depth * wide, bytes_accessed=2 * depth * wide, transcendentals=0
         ),
     )(context, weights, middle)
+
+
+def relay_kernel(a_ref, b_ref, out_ref, *, tail):
+    wide = a_ref.shape[1] - tail
+    out_ref[:, :wide] = (a_ref[:, :wide].astype(F32) + b_ref[:, :wide].astype(F32)).astype(BF16)
+    half = tail // 2
+    ends = a_ref[:, wide:].astype(F32) + b_ref[:, wide:].astype(F32)
+    total = ends[:, :half] + ends[:, half:]
+    high = total.astype(BF16)
+    low = (total - high.astype(F32)).astype(BF16)
+    out_ref[:, wide:] = jnp.concatenate([high, low], axis=1)
+
+
+def add_pieces(a, b, tail):
+    vmem = pl.BlockSpec(memory_space=pltpu.VMEM)
+    return pl.pallas_call(
+        functools.partial(relay_kernel, tail=tail),
+        in_specs=[vmem, vmem],
+        out_specs=vmem,
+        out_shape=jax.ShapeDtypeStruct(a.shape, BF16),
+        compiler_params=params(4),
+        name="relay",
+    )(a, b)
 
 
 def final_kernel(own_ref, pm_ref, up_ref, *refs):
@@ -534,15 +577,31 @@
         parts.append(hop(part, "tp", k))
     q_up, od, out_up, k_up, v_up = assemble(up_blocks, widths)
     far = tp - 1
+    first = LINE[0] if tp == 4 else far
     context, middle, piece = attention(
         lengths, base_q, base_kv, parts, (q_up, k_up, v_up), od, (cosine, sine),
-        cache_keys, cache_values, output_weight_matrix, far,
+        cache_keys, cache_values, output_weight_matrix, first,
     )
-    others = [hop(piece, "tp", far)]
-    for k in range(far - 1, 0, -1):
-        piece = chunk(context, output_weight_matrix, middle, k)
-        others.append(hop(piece, "tp", k))
-    own = chunk(context, output_weight_matrix, middle, 0)
+
+    def made(target):
+        return chunk(context, output_weight_matrix, middle, target)
+
+    def sent(x, pairs):
+        return lax.ppermute(x, "tp", pairs)
+
+    if tp == 4:
+        across = sent(piece, [(1, 2), (2, 1)])
+        relayed = sent(piece, [(0, 1), (3, 2)])
+        piece = made(LINE[1])
+        second = sent(piece, [(0, 2), (1, 0), (2, 3), (3, 1)])
+        piece = made(LINE[2])
+        piece = add_pieces(piece, relayed, middle.shape[1])
+        others = [across, second, sent(piece, [(0, 1), (1, 3), (2, 0), (3, 2)])]
+    else:
+        others = [hop(piece, "tp", far)]
+        for k in range(far - 1, 0, -1):
+            others.append(hop(made(k), "tp", k))
+    own = made(0)
     return finish(own, middle, out_up, others)
 
 

time: 71.2 us -> 66.6 us (0.935)
  the two profiles are of different devices: /device:TPU:15 before, /device:TPU:0 now
where the time goes in v2:
time: 66.6 us; the launch traced here: 66.4 us
  starting transfers between devices  25.8 us (39%)
  Pallas kernels  19.1 us (29%)
  waiting for transfers between devices  18.2 us (27%)
  local copies, waits for them, and re-layouts  3.11 us (5%)
    ppermute x17, starting transfers between devices, hop(): return lax.ppermute(x, axis, [(i, to(i, k)) for i in range(n)])  16.5 us
    ppermute x4, waiting for transfers between devices, sent(): return lax.ppermute(x, 'tp', pairs)  10.7 us
    ppermute x4, starting transfers between devices, sent(): return lax.ppermute(x, 'tp', pairs)  8.55 us
    ppermute x17, waiting for transfers between devices, hop(): return lax.ppermute(x, axis, [(i, to(i, k)) for i in range(n)])  7.44 us
    pallas_call x1, Pallas kernels, base_projections(): pl.pallas_call(base_kernel, in_specs=[vmem] * 4, out_specs=[vmem] * 3, ou...  6.8 us
    pallas_call x1, Pallas kernels, attention(): pl.pallas_call(functools.partial(attend_kernel, parts=len(parts), group=h...  5.86 us
    pallas_call x3, Pallas kernels, chunk(): pl.pallas_call(functools.partial(chunk_kernel, k=k), in_specs=[vmem, vmem...  3.65 us
    unnamed x32, local copies, waits for them, and re-layouts  3.11 us
  transfers between devices with their start and end apart: 22, of which 8 were waited for; matrix products, arithmetic and copies ran while one was open for 0% of the time, Pallas kernels for 18%

profile of v2, /device:TPU:0, one launch (start us, length us, event | category | flops | bytes accessed | tf_op | source)
XLA Modules:
  0.0 66.4 jit_solution(9600621140381804487)
XLA Ops:
  0.0 0.0 copy-start.8
  0.1 0.8 %copy-done.10 = bf16[3,256,64]{1,2,0:T(8,128)(2,1)S(1)} copy-done((bf16[3,256,64]{1,2,0:T(8,128)(2,1)S(1)}, bf16[3,256,64]{1,2,0:T(8,128)(2,1)}, u32[]{:S(2)}) %copy-start.10) | copy-done | bytes 98328
  0.9 0.5 collective-permute-start.11
  1.4 3.4 %collective-permute-start.10 = (bf16[192,256]{1,0:T(8,128)(2,1)S(1)}, bf16[192,256]{1,0:T(8,128)(2,1)S(1)}, u32[]{:S(2)}, u32[]{:S(2)}) collective-permute-start(bf16[192,256]{1,0:T(8,128)(2,1)S(1)} %bitcast.11), channel_id=1, source_target_pairs={{0,24},{4,28},{8,16},{12,20},{16,8},{20,12},{24,0},{28,4},{1,25},{... | collective-permute-start | bytes 294920 | tf_op jit(solution)/shard_map/ppermute | solution.py:45
  4.8 0.5 collective-permute-start.9
  5.3 0.1 collective-permute-start.8
  5.4 0.0 copy-done.4
  5.4 0.1 pack.1
  5.5 0.8 %collective-permute-start = (bf16[64,576]{1,0:T(8,128)(2,1)S(1)}, bf16[64,576]{1,0:T(8,128)(2,1)S(1)}, u32[]{:S(2)}, u32[]{:S(2)}) collective-permute-start(bf16[64,576]{1,0:T(8,128)(2,1)S(1)} %pack.1), channel_id=1, source_target_pairs={{0,0},{1,4},{2,8},{3,12},{4,16},{5,20},{6,24},{7,28},{8,1},{9,5},{... | collective-permute-start | bytes 221192 | tf_op jit(solution)/shard_map/ppermute | solution.py:566
  6.3 2.0 %copy-done.7 = bf16[8192,1024]{1,0:T(8,128)(2,1)S(1)} copy-done((bf16[8192,1024]{1,0:T(8,128)(2,1)S(1)}, bf16[8192,1024]{1,0:T(8,128)(2,1)}, u32[]{:S(2)}) %copy-start.7) | copy-done | bytes 16777240
  8.3 0.2 copy-done.9
  8.5 6.8 %base.1 = (bf16[64,8192]{1,0:T(8,128)(2,1)S(1)}, f32[64,1024]{1,0:T(8,128)S(1)}, f32[2,64,256]{2,1,0:T(8,128)S(1)}) custom-call(bf16[64,128]{1,0:T(8,128)(2,1)S(1)} %bitcast.15, bf16[64,8192]{1,0:T(8,128)(2,1)S(1)} %copy-done.9, bf16[8192,1024]{1,0:T(8,128)(2,1)S(1)} %copy-done.7, bf16[2,8192,256]{2,1,0:T(8,128)(2,1)S(1)} %copy-done.8), custom_call_target="tpu_custom_call" | custom-call | flops 12884901888 | bytes 25165824 | tf_op jit(solution)/shard_map/base/pallas_call | solution.py:191
  15.3 0.0 collective-permute-done.refs_0_
  15.4 5.7 %collective-permute-start.3 = (bf16[64,576]{1,0:T(8,128)(2,1)S(1)}, bf16[64,576]{1,0:T(8,128)(2,1)S(1)}, u32[]{:S(2)}, u32[]{:S(2)}) collective-permute-start(bf16[64,576]{1,0:T(8,128)(2,1)S(1)} %collective-permute-done.refs_0_), channel_id=1, source_target_pairs={{0,24},{4,28},{8,16},{12,20},{16,8},{20,12},{24,0},{28,4},{1,25},{... | collective-permute-start | bytes 221192 | tf_op jit(solution)/shard_map/ppermute | solution.py:45
  21.1 0.0 collective-permute-done.10.refs_3_
  21.1 0.0 collective-permute-start.14
  21.1 0.0 collective-permute-done.9.refs_2_
  21.1 0.5 collective-permute-start.13
  21.6 0.0 collective-permute-done.8.refs_1_
  21.6 0.1 collective-permute-start.12
  21.7 0.0 collective-permute-done.11.refs_4_
  21.7 0.0 collective-permute-start.2
  21.7 2.2 %collective-permute-done.3.refs_3_ = bf16[64,576]{1,0:T(8,128)(2,1)S(1)} collective-permute-done((bf16[64,576]{1,0:T(8,128)(2,1)S(1)}, bf16[64,576]{1,0:T(8,128)(2,1)S(1)}, u32[]{:S(2)}, u32[]{:S(2)}) %collective-permute-start.3) | collective-permute-done | bytes 73760 | tf_op jit(solution)/shard_map/ppermute | solution.py:45
  23.9 0.6 collective-permute-start.1
  24.5 2.0 %collective-permute-done.2.refs_2_ = bf16[64,576]{1,0:T(8,128)(2,1)S(1)} collective-permute-done((bf16[64,576]{1,0:T(8,128)(2,1)S(1)}, bf16[64,576]{1,0:T(8,128)(2,1)S(1)}, u32[]{:S(2)}, u32[]{:S(2)}) %collective-permute-start.2) | collective-permute-done | bytes 73760 | tf_op jit(solution)/shard_map/ppermute | solution.py:45
  26.5 0.0 collective-permute-start.4
  26.5 1.8 %collective-permute-done.1.refs_1_ = bf16[64,576]{1,0:T(8,128)(2,1)S(1)} collective-permute-done((bf16[64,576]{1,0:T(8,128)(2,1)S(1)}, bf16[64,576]{1,0:T(8,128)(2,1)S(1)}, u32[]{:S(2)}, u32[]{:S(2)}) %collective-permute-start.1) | collective-permute-done | bytes 73760 | tf_op jit(solution)/shard_map/ppermute | solution.py:45
  28.3 0.0 collective-permute-start.7
  28.3 0.0 collective-permute-done.14.refs_7_
  28.3 0.5 collective-permute-start.6
  28.8 0.0 collective-permute-done.13.refs_6_
  28.8 0.1 collective-permute-start.5
  28.9 0.0 collective-permute-done.12.refs_5_
  28.9 0.0 copy-start.1
  28.9 0.4 inner.1.refs_0_
  29.3 2.1 %collective-permute-start.17 = (bf16[64,256]{1,0:T(8,128)(2,1)S(1)}, bf16[64,256]{1,0:T(8,128)(2,1)S(1)}, u32[]{:S(2)}, u32[]{:S(2)}) collective-permute-start(bf16[64,256]{1,0:T(8,128)(2,1)S(1)} %inner.1.refs_0_), channel_id=1, source_target_pairs={{0,3},{1,2},{2,1},{3,0},{4,7},{5,6},{6,5},{7,4},{8,11},{9,10},{10,... | collective-permute-start | bytes 98312 | tf_op jit(solution)/shard_map/ppermute | solution.py:45
  31.3 0.0 collective-permute-done.4.refs_4_
  31.3 0.0 collective-permute-start.16
  31.3 0.0 collective-permute-done.7.refs_7_
  31.4 2.4 %collective-permute-start.15 = (bf16[64,256]{1,0:T(8,128)(2,1)S(1)}, bf16[64,256]{1,0:T(8,128)(2,1)S(1)}, u32[]{:S(2)}, u32[]{:S(2)}) collective-permute-start(bf16[64,256]{1,0:T(8,128)(2,1)S(1)} %inner.1.refs_0_), channel_id=1, source_target_pairs={{0,1},{1,0},{2,3},{3,2},{4,5},{5,4},{6,7},{7,6},{8,9},{9,8},{10,11... | collective-permute-start | bytes 98312 | tf_op jit(solution)/shard_map/ppermute | solution.py:45
  33.7 0.8 %tables.1 = (f32[64,128]{1,0:T(8,128)S(1)}, f32[64,128]{1,0:T(8,128)S(1)}) custom-call(s32[64]{0:T(128)S(1)} %copy-done.6, f32[8,128]{1,0:T(8,128)S(1)} %opening.1._), custom_call_target="tpu_custom_call" | custom-call | tf_op jit(solution)/shard_map/tables/pallas_call | solution.py:146
  34.5 0.0 collective-permute-done.6.refs_6_
  34.5 0.0 collective-permute-done.5.refs_5_
  34.5 0.3 assemble.1
  34.9 0.4 collective-permute-done.17.refs_3_
  35.3 1.0 %collective-permute-done.16.refs_2_ = bf16[64,256]{1,0:T(8,128)(2,1)S(1)} collective-permute-done((bf16[64,256]{1,0:T(8,128)(2,1)S(1)}, bf16[64,256]{1,0:T(8,128)(2,1)S(1)}, u32[]{:S(2)}, u32[]{:S(2)}) %collective-permute-start.16) | collective-permute-done | bytes 32800 | tf_op jit(solution)/shard_map/ppermute | solution.py:45
  36.3 0.0 collective-permute-done.15.refs_1_
  36.3 0.0 slice-done.3
  36.3 0.0 copy-done
  36.3 0.0 copy-done.1
  36.4 5.9 %attend.1 = (bf16[64,1024]{1,0:T(8,128)(2,1)S(1)}, bf16[64,128]{1,0:T(8,128)(2,1)S(1)}, bf16[64,2176]{1,0:T(8,128)(2,1)S(1)}) custom-call(s32[64]{0:T(128)S(1)} %copy-done.6, f32[64,1024]{1,0:T(8,128)S(1)} %get-tuple-element.23.q_ref, f32[2,64,256]{2,1,0:T(8,128)S(1)} %get-tuple-element.24.kv_ref, bf16[64,1024]{1,0:T(8,128)(2,1)S(1)} %get-tuple-element.26.q_up, ...), custom_call_target="tpu_custom_call" | custom-call | flops 536870912 | bytes 8388608 | tf_op jit(solution)/shard_map/attend/pallas_call | solution.py:426
  42.2 3.3 %collective-permute-start.20 = (bf16[64,2176]{1,0:T(8,128)(2,1)S(1)}, bf16[64,2176]{1,0:T(8,128)(2,1)S(1)}, u32[]{:S(2)}, u32[]{:S(2)}) collective-permute-start(bf16[64,2176]{1,0:T(8,128)(2,1)S(1)} %get-tuple-element.38), channel_id=1, source_target_pairs={{0,1},{3,2},{4,5},{7,6},{8,9},{11,10},{12,13},{15,14},{16,17},{19,... | collective-permute-start | bytes 835592 | tf_op jit(solution)/shard_map/ppermute | solution.py:590
  45.5 0.7 %collective-permute-start.18 = (bf16[64,2176]{1,0:T(8,128)(2,1)S(1)}, bf16[64,2176]{1,0:T(8,128)(2,1)S(1)}, u32[]{:S(2)}, u32[]{:S(2)}) collective-permute-start(bf16[64,2176]{1,0:T(8,128)(2,1)S(1)} %get-tuple-element.38), channel_id=1, source_target_pairs={{1,2},{2,1},{5,6},{6,5},{9,10},{10,9},{13,14},{14,13},{17,18},{18,... | collective-permute-start | bytes 835592 | tf_op jit(solution)/shard_map/ppermute | solution.py:590
  46.2 1.2 %shard_map.128 = bf16[64,2176]{1,0:T(8,128)(2,1)S(1)} custom-call(bf16[64,1024]{1,0:T(8,128)(2,1)S(1)} %get-tuple-element.35.ctx_ref, bf16[1024,8192]{1,0:T(8,128)(2,1)S(1)} %bitcast.7, bf16[64,128]{1,0:T(8,128)(2,1)S(1)} %get-tuple-element.36.pm_ref), custom_call_target="tpu_custom_call" | custom-call | flops 268435456 | bytes 4194304 | tf_op jit(solution)/shard_map/pallas_call | solution.py:475
  47.4 2.1 %collective-permute-start.19 = (bf16[64,2176]{1,0:T(8,128)(2,1)S(1)}, bf16[64,2176]{1,0:T(8,128)(2,1)S(1)}, u32[]{:S(2)}, u32[]{:S(2)}) collective-permute-start(bf16[64,2176]{1,0:T(8,128)(2,1)S(1)} %shard_map.128), channel_id=1, source_target_pairs={{0,2},{1,0},{2,3},{3,1},{4,6},{5,4},{6,7},{7,5},{8,10},{9,8},{10,1... | collective-permute-start | bytes 835592 | tf_op jit(solution)/shard_map/ppermute | solution.py:590
  49.5 1.2 %shard_map.129.a_ref = bf16[64,2176]{1,0:T(8,128)(2,1)S(1)} custom-call(bf16[64,1024]{1,0:T(8,128)(2,1)S(1)} %get-tuple-element.35.ctx_ref, bf16[1024,8192]{1,0:T(8,128)(2,1)S(1)} %bitcast.7, bf16[64,128]{1,0:T(8,128)(2,1)S(1)} %get-tuple-element.36.pm_ref), custom_call_target="tpu_custom_call" | custom-call | flops 268435456 | bytes 4194304 | tf_op jit(solution)/shard_map/pallas_call | solution.py:475
  50.8 1.7 %collective-permute-done.20.b_ref = bf16[64,2176]{1,0:T(8,128)(2,1)S(1)} collective-permute-done((bf16[64,2176]{1,0:T(8,128)(2,1)S(1)}, bf16[64,2176]{1,0:T(8,128)(2,1)S(1)}, u32[]{:S(2)}, u32[]{:S(2)}) %collective-permute-start.20) | collective-permute-done | bytes 278560 | tf_op jit(solution)/shard_map/ppermute | solution.py:590
  52.4 0.2 relay.1
  52.7 2.5 %collective-permute-start.21 = (bf16[64,2176]{1,0:T(8,128)(2,1)S(1)}, bf16[64,2176]{1,0:T(8,128)(2,1)S(1)}, u32[]{:S(2)}, u32[]{:S(2)}) collective-permute-start(bf16[64,2176]{1,0:T(8,128)(2,1)S(1)} %relay.1), channel_id=1, source_target_pairs={{0,1},{1,3},{2,0},{3,2},{4,5},{5,7},{6,4},{7,6},{8,9},{9,11},{10,8... | collective-permute-start | bytes 835592 | tf_op jit(solution)/shard_map/ppermute | solution.py:590
  55.2 1.2 %shard_map.127.own_ref = f32[64,2048]{1,0:T(8,128)S(1)} custom-call(bf16[64,1024]{1,0:T(8,128)(2,1)S(1)} %get-tuple-element.35.ctx_ref, bf16[1024,8192]{1,0:T(8,128)(2,1)S(1)} %bitcast.7, bf16[64,128]{1,0:T(8,128)(2,1)S(1)} %get-tuple-element.36.pm_ref), custom_call_target="tpu_custom_call" | custom-call | flops 268435456 | bytes 4194304 | tf_op jit(solution)/shard_map/pallas_call | solution.py:475
  56.4 2.1 %collective-permute-done.19.refs_1_ = bf16[64,2176]{1,0:T(8,128)(2,1)S(1)} collective-permute-done((bf16[64,2176]{1,0:T(8,128)(2,1)S(1)}, bf16[64,2176]{1,0:T(8,128)(2,1)S(1)}, u32[]{:S(2)}, u32[]{:S(2)}) %collective-permute-start.19) | collective-permute-done | bytes 278560 | tf_op jit(solution)/shard_map/ppermute | solution.py:590
  58.5 0.0 collective-permute-done.18.refs_0_
  58.5 7.0 %collective-permute-done.21.refs_2_ = bf16[64,2176]{1,0:T(8,128)(2,1)S(1)} collective-permute-done((bf16[64,2176]{1,0:T(8,128)(2,1)S(1)}, bf16[64,2176]{1,0:T(8,128)(2,1)S(1)}, u32[]{:S(2)}, u32[]{:S(2)}) %collective-permute-start.21) | collective-permute-done | bytes 278560 | tf_op jit(solution)/shard_map/ppermute | solution.py:590
  65.4 1.0 %final.1 = bf16[64,2048]{1,0:T(8,128)(2,1)} custom-call(f32[64,2048]{1,0:T(8,128)S(1)} %shard_map.127.own_ref, bf16[64,128]{1,0:T(8,128)(2,1)S(1)} %get-tuple-element.36.pm_ref, bf16[64,2048]{1,0:T(8,128)(2,1)S(1)} %get-tuple-element.37.up_ref, bf16[64,2176]{1,0:T(8,128)(2,1)S(1)} %collective-permute-done.18.refs_0_, ...), custom_call_target="tpu_custom_call" | custom-call | tf_op jit(solution)/shard_map/final/pallas_call | solution.py:528
  (25 shorter events, 0.0 us)
Async XLA Ops:
  0.0 0.9 %copy-start.10 = (bf16[3,256,64]{1,2,0:T(8,128)(2,1)S(1)}, bf16[3,256,64]{1,2,0:T(8,128)(2,1)}, u32[]{:S(2)}) copy-start(bf16[3,256,64]{1,2,0:T(8,128)(2,1)} %param.18) | copy-start | bytes 294916
  0.0 5.4 %copy-start.2 = (bf16[64,256]{1,0:T(8,128)(2,1)S(1)}, bf16[64,256]{1,0:T(8,128)(2,1)}, u32[]{:S(2)}) copy-start(bf16[64,256]{1,0:T(8,128)(2,1)} %ou_ref.1) | copy-start | bytes 98308
  0.0 5.4 %copy-start.4 = (bf16[128,64]{0,1:T(8,128)(2,1)S(1)}, bf16[128,64]{0,1:T(8,128)(2,1)}, u32[]{:S(2)}) copy-start(bf16[128,64]{0,1:T(8,128)(2,1)} %param.21) | copy-start | bytes 49156
  0.0 5.4 %copy-start.5 = (bf16[2,64,32]{1,2,0:T(8,128)(2,1)S(1)}, bf16[2,64,32]{1,2,0:T(8,128)(2,1)}, u32[]{:S(2)}) copy-start(bf16[2,64,32]{1,2,0:T(8,128)(2,1)} %param.20) | copy-start | bytes 24580
  0.0 5.4 %copy-start.3 = (bf16[64,128]{1,0:T(8,128)(2,1)S(1)}, bf16[64,128]{1,0:T(8,128)(2,1)}, u32[]{:S(2)}) copy-start(bf16[64,128]{1,0:T(8,128)(2,1)} %q_ref.1) | copy-start | bytes 49156
  0.0 6.3 %copy-start.8 = (bf16[2,8192,256]{2,1,0:T(8,128)(2,1)S(1)}, bf16[2,8192,256]{2,1,0:T(8,128)(2,1)}, u32[]{:S(2)}) copy-start(bf16[2,8192,256]{2,1,0:T(8,128)(2,1)} %kv_held.1) | copy-start | bytes 25165828
  0.0 8.3 %copy-start.7 = (bf16[8192,1024]{1,0:T(8,128)(2,1)S(1)}, bf16[8192,1024]{1,0:T(8,128)(2,1)}, u32[]{:S(2)}) copy-start(bf16[8192,1024]{1,0:T(8,128)(2,1)} %q_held.1) | copy-start | bytes 50331652
  0.0 8.3 %copy-start.11 = (bf16[8192]{0:T(1024)(128)(2,1)S(1)}, bf16[8192]{0:T(1024)(128)(2,1)}, u32[]{:S(2)}) copy-start(bf16[8192]{0:T(1024)(128)(2,1)} %param.14) | copy-start | bytes 49156
  0.0 8.5 %copy-start.9 = (bf16[64,8192]{1,0:T(8,128)(2,1)S(1)}, bf16[64,8192]{1,0:T(8,128)(2,1)}, u32[]{:S(2)}) copy-start(bf16[64,8192]{1,0:T(8,128)(2,1)} %hidden.1) | copy-start | bytes 3145732
  0.9 20.8 %collective-permute-start.11 = (bf16[192,256]{1,0:T(8,128)(2,1)S(1)}, bf16[192,256]{1,0:T(8,128)(2,1)S(1)}, u32[]{:S(2)}, u32[]{:S(2)}) collective-permute-start(bf16[192,256]{1,0:T(8,128)(2,1)S(1)} %bitcast.10), channel_id=1, source_target_pairs={{0,4},{4,0},{8,12},{12,8},{16,20},{20,16},{24,28},{28,24},{1,5},{5... | collective-permute-start | bytes 294920 | tf_op jit(solution)/shard_map/ppermute | solution.py:45
  1.4 19.7 %collective-permute-start.10 = (bf16[192,256]{1,0:T(8,128)(2,1)S(1)}, bf16[192,256]{1,0:T(8,128)(2,1)S(1)}, u32[]{:S(2)}, u32[]{:S(2)}) collective-permute-start(bf16[192,256]{1,0:T(8,128)(2,1)S(1)} %bitcast.11), channel_id=1, source_target_pairs={{0,24},{4,28},{8,16},{12,20},{16,8},{20,12},{24,0},{28,4},{1,25},{... | collective-permute-start | bytes 294920 | tf_op jit(solution)/shard_map/ppermute | solution.py:45
  4.8 16.3 %collective-permute-start.9 = (bf16[192,256]{1,0:T(8,128)(2,1)S(1)}, bf16[192,256]{1,0:T(8,128)(2,1)S(1)}, u32[]{:S(2)}, u32[]{:S(2)}) collective-permute-start(bf16[192,256]{1,0:T(8,128)(2,1)S(1)} %bitcast.12), channel_id=1, source_target_pairs={{0,16},{4,20},{8,24},{12,28},{16,0},{20,4},{24,8},{28,12},{1,17},{... | collective-permute-start | bytes 294920 | tf_op jit(solution)/shard_map/ppermute | solution.py:45
  5.3 16.3 %collective-permute-start.8 = (bf16[192,256]{1,0:T(8,128)(2,1)S(1)}, bf16[192,256]{1,0:T(8,128)(2,1)S(1)}, u32[]{:S(2)}, u32[]{:S(2)}) collective-permute-start(bf16[192,256]{1,0:T(8,128)(2,1)S(1)} %bitcast.13), channel_id=1, source_target_pairs={{0,8},{4,12},{8,0},{12,4},{16,24},{20,28},{24,16},{28,20},{1,9},{5... | collective-permute-start | bytes 294920 | tf_op jit(solution)/shard_map/ppermute | solution.py:45
  5.5 9.9 %collective-permute-start = (bf16[64,576]{1,0:T(8,128)(2,1)S(1)}, bf16[64,576]{1,0:T(8,128)(2,1)S(1)}, u32[]{:S(2)}, u32[]{:S(2)}) collective-permute-start(bf16[64,576]{1,0:T(8,128)(2,1)S(1)} %pack.1), channel_id=1, source_target_pairs={{0,0},{1,4},{2,8},{3,12},{4,16},{5,20},{6,24},{7,28},{8,1},{9,5},{... | collective-permute-start | bytes 221192 | tf_op jit(solution)/shard_map/ppermute | solution.py:566
  8.5 27.8 %slice-start = ((s8[16777216]{0:T(1024)(128)(4,1)}), s8[4194304]{0:T(1024)(128)(4,1)S(1)}, s32[]{:S(2)}) async-start(s8[16777216]{0:T(1024)(128)(4,1)} %bitcast.6), calls=%async_computation | async-start | bytes 8388608
  8.5 27.8 %slice-start.1 = ((s8[16777216]{0:T(1024)(128)(4,1)}), s8[4194304]{0:T(1024)(128)(4,1)S(1)}, s32[]{:S(2)}) async-start(s8[16777216]{0:T(1024)(128)(4,1)} %bitcast.6), calls=%async_computation.1 | async-start | bytes 8388608
  8.5 27.8 %slice-start.2 = ((s8[16777216]{0:T(1024)(128)(4,1)}), s8[4194304]{0:T(1024)(128)(4,1)S(1)}, s32[]{:S(2)}) async-start(s8[16777216]{0:T(1024)(128)(4,1)} %bitcast.6), calls=%async_computation.2 | async-start | bytes 8388608
  15.4 8.5 %collective-permute-start.3 = (bf16[64,576]{1,0:T(8,128)(2,1)S(1)}, bf16[64,576]{1,0:T(8,128)(2,1)S(1)}, u32[]{:S(2)}, u32[]{:S(2)}) collective-permute-start(bf16[64,576]{1,0:T(8,128)(2,1)S(1)} %collective-permute-done.refs_0_), channel_id=1, source_target_pairs={{0,24},{4,28},{8,16},{12,20},{16,8},{20,12},{24,0},{28,4},{1,25},{... | collective-permute-start | bytes 221192 | tf_op jit(solution)/shard_map/ppermute | solution.py:45
  21.1 7.2 %collective-permute-start.14 = (bf16[192,256]{1,0:T(8,128)(2,1)S(1)}, bf16[192,256]{1,0:T(8,128)(2,1)S(1)}, u32[]{:S(2)}, u32[]{:S(2)}) collective-permute-start(bf16[192,256]{1,0:T(8,128)(2,1)S(1)} %collective-permute-done.10.refs_3_), channel_id=1, source_target_pairs={{0,4},{4,0},{8,12},{12,8},{16,20},{20,16},{24,28},{28,24},{1,5},{5... | collective-permute-start | bytes 294920 | tf_op jit(solution)/shard_map/ppermute | solution.py:45
  21.1 7.7 %collective-permute-start.13 = (bf16[192,256]{1,0:T(8,128)(2,1)S(1)}, bf16[192,256]{1,0:T(8,128)(2,1)S(1)}, u32[]{:S(2)}, u32[]{:S(2)}) collective-permute-start(bf16[192,256]{1,0:T(8,128)(2,1)S(1)} %collective-permute-done.9.refs_2_), channel_id=1, source_target_pairs={{0,4},{4,0},{8,12},{12,8},{16,20},{20,16},{24,28},{28,24},{1,5},{5... | collective-permute-start | bytes 294920 | tf_op jit(solution)/shard_map/ppermute | solution.py:45
  21.6 7.3 %collective-permute-start.12 = (bf16[192,256]{1,0:T(8,128)(2,1)S(1)}, bf16[192,256]{1,0:T(8,128)(2,1)S(1)}, u32[]{:S(2)}, u32[]{:S(2)}) collective-permute-start(bf16[192,256]{1,0:T(8,128)(2,1)S(1)} %collective-permute-done.8.refs_1_), channel_id=1, source_target_pairs={{0,4},{4,0},{8,12},{12,8},{16,20},{20,16},{24,28},{28,24},{1,5},{5... | collective-permute-start | bytes 294920 | tf_op jit(solution)/shard_map/ppermute | solution.py:45
  21.7 4.8 %collective-permute-start.2 = (bf16[64,576]{1,0:T(8,128)(2,1)S(1)}, bf16[64,576]{1,0:T(8,128)(2,1)S(1)}, u32[]{:S(2)}, u32[]{:S(2)}) collective-permute-start(bf16[64,576]{1,0:T(8,128)(2,1)S(1)} %collective-permute-done.refs_0_), channel_id=1, source_target_pairs={{0,16},{4,20},{8,24},{12,28},{16,0},{20,4},{24,8},{28,12},{1,17},{... | collective-permute-start | bytes 221192 | tf_op jit(solution)/shard_map/ppermute | solution.py:45
  23.9 4.4 %collective-permute-start.1 = (bf16[64,576]{1,0:T(8,128)(2,1)S(1)}, bf16[64,576]{1,0:T(8,128)(2,1)S(1)}, u32[]{:S(2)}, u32[]{:S(2)}) collective-permute-start(bf16[64,576]{1,0:T(8,128)(2,1)S(1)} %collective-permute-done.refs_0_), channel_id=1, source_target_pairs={{0,8},{4,12},{8,0},{12,4},{16,24},{20,28},{24,16},{28,20},{1,9},{5... | collective-permute-start | bytes 221192 | tf_op jit(solution)/shard_map/ppermute | solution.py:45
  26.5 4.9 %collective-permute-start.4 = (bf16[64,576]{1,0:T(8,128)(2,1)S(1)}, bf16[64,576]{1,0:T(8,128)(2,1)S(1)}, u32[]{:S(2)}, u32[]{:S(2)}) collective-permute-start(bf16[64,576]{1,0:T(8,128)(2,1)S(1)} %collective-permute-done.refs_0_), channel_id=1, source_target_pairs={{0,4},{4,0},{8,12},{12,8},{16,20},{20,16},{24,28},{28,24},{1,5},{5... | collective-permute-start | bytes 221192 | tf_op jit(solution)/shard_map/ppermute | solution.py:45
  28.3 3.1 %collective-permute-start.7 = (bf16[64,576]{1,0:T(8,128)(2,1)S(1)}, bf16[64,576]{1,0:T(8,128)(2,1)S(1)}, u32[]{:S(2)}, u32[]{:S(2)}) collective-permute-start(bf16[64,576]{1,0:T(8,128)(2,1)S(1)} %collective-permute-done.3.refs_3_), channel_id=1, source_target_pairs={{0,4},{4,0},{8,12},{12,8},{16,20},{20,16},{24,28},{28,24},{1,5},{5... | collective-permute-start | bytes 221192 | tf_op jit(solution)/shard_map/ppermute | solution.py:45
  28.3 6.2 %collective-permute-start.6 = (bf16[64,576]{1,0:T(8,128)(2,1)S(1)}, bf16[64,576]{1,0:T(8,128)(2,1)S(1)}, u32[]{:S(2)}, u32[]{:S(2)}) collective-permute-start(bf16[64,576]{1,0:T(8,128)(2,1)S(1)} %collective-permute-done.2.refs_2_), channel_id=1, source_target_pairs={{0,4},{4,0},{8,12},{12,8},{16,20},{20,16},{24,28},{28,24},{1,5},{5... | collective-permute-start | bytes 221192 | tf_op jit(solution)/shard_map/ppermute | solution.py:45
  28.8 5.7 %collective-permute-start.5 = (bf16[64,576]{1,0:T(8,128)(2,1)S(1)}, bf16[64,576]{1,0:T(8,128)(2,1)S(1)}, u32[]{:S(2)}, u32[]{:S(2)}) collective-permute-start(bf16[64,576]{1,0:T(8,128)(2,1)S(1)} %collective-permute-done.1.refs_1_), channel_id=1, source_target_pairs={{0,4},{4,0},{8,12},{12,8},{16,20},{20,16},{24,28},{28,24},{1,5},{5... | collective-permute-start | bytes 221192 | tf_op jit(solution)/shard_map/ppermute | solution.py:45
  28.9 4.9 %copy-start.6 = (s32[64]{0:T(128)S(1)}, s32[64]{0:T(128)}, u32[]{:S(2)}) copy-start(s32[64]{0:T(128)} %lengths_ref.3) | copy-start | bytes 772
  28.9 7.4 %slice-start.3 = ((s8[16777216]{0:T(1024)(128)(4,1)}), s8[4194304]{0:T(1024)(128)(4,1)S(1)}, s32[]{:S(2)}) async-start(s8[16777216]{0:T(1024)(128)(4,1)} %bitcast.6), calls=%async_computation.3 | async-start | bytes 8388608
  28.9 7.4 %copy-start = (bf16[64,2,128,128]{3,2,1,0:T(8,128)(2,1)S(1)}, bf16[64,2,128,128]{3,2,1,0:T(8,128)(2,1)}, u32[]{:S(2)}) copy-start(bf16[64,2,128,128]{3,2,1,0:T(8,128)(2,1)} %refs_4_.1) | copy-start | bytes 12582916
  28.9 7.4 %copy-start.1 = (bf16[64,2,128,128]{3,2,1,0:T(8,128)(2,1)S(1)}, bf16[64,2,128,128]{3,2,1,0:T(8,128)(2,1)}, u32[]{:S(2)}) copy-start(bf16[64,2,128,128]{3,2,1,0:T(8,128)(2,1)} %refs_5_.1) | copy-start | bytes 12582916
  29.3 6.0 %collective-permute-start.17 = (bf16[64,256]{1,0:T(8,128)(2,1)S(1)}, bf16[64,256]{1,0:T(8,128)(2,1)S(1)}, u32[]{:S(2)}, u32[]{:S(2)}) collective-permute-start(bf16[64,256]{1,0:T(8,128)(2,1)S(1)} %inner.1.refs_0_), channel_id=1, source_target_pairs={{0,3},{1,2},{2,1},{3,0},{4,7},{5,6},{6,5},{7,4},{8,11},{9,10},{10,... | collective-permute-start | bytes 98312 | tf_op jit(solution)/shard_map/ppermute | solution.py:45
  31.3 4.9 %collective-permute-start.16 = (bf16[64,256]{1,0:T(8,128)(2,1)S(1)}, bf16[64,256]{1,0:T(8,128)(2,1)S(1)}, u32[]{:S(2)}, u32[]{:S(2)}) collective-permute-start(bf16[64,256]{1,0:T(8,128)(2,1)S(1)} %inner.1.refs_0_), channel_id=1, source_target_pairs={{0,2},{1,3},{2,0},{3,1},{4,6},{5,7},{6,4},{7,5},{8,10},{9,11},{10,... | collective-permute-start | bytes 98312 | tf_op jit(solution)/shard_map/ppermute | solution.py:45
  31.4 5.0 %collective-permute-start.15 = (bf16[64,256]{1,0:T(8,128)(2,1)S(1)}, bf16[64,256]{1,0:T(8,128)(2,1)S(1)}, u32[]{:S(2)}, u32[]{:S(2)}) collective-permute-start(bf16[64,256]{1,0:T(8,128)(2,1)S(1)} %inner.1.refs_0_), channel_id=1, source_target_pairs={{0,1},{1,0},{2,3},{3,2},{4,5},{5,4},{6,7},{7,6},{8,9},{9,8},{10,11... | collective-permute-start | bytes 98312 | tf_op jit(solution)/shard_map/ppermute | solution.py:45
  42.2 10.2 %collective-permute-start.20 = (bf16[64,2176]{1,0:T(8,128)(2,1)S(1)}, bf16[64,2176]{1,0:T(8,128)(2,1)S(1)}, u32[]{:S(2)}, u32[]{:S(2)}) collective-permute-start(bf16[64,2176]{1,0:T(8,128)(2,1)S(1)} %get-tuple-element.38), channel_id=1, source_target_pairs={{0,1},{3,2},{4,5},{7,6},{8,9},{11,10},{12,13},{15,14},{16,17},{19,... | collective-permute-start | bytes 835592 | tf_op jit(solution)/shard_map/ppermute | solution.py:590
  45.5 13.0 %collective-permute-start.18 = (bf16[64,2176]{1,0:T(8,128)(2,1)S(1)}, bf16[64,2176]{1,0:T(8,128)(2,1)S(1)}, u32[]{:S(2)}, u32[]{:S(2)}) collective-permute-start(bf16[64,2176]{1,0:T(8,128)(2,1)S(1)} %get-tuple-element.38), channel_id=1, source_target_pairs={{1,2},{2,1},{5,6},{6,5},{9,10},{10,9},{13,14},{14,13},{17,18},{18,... | collective-permute-start | bytes 835592 | tf_op jit(solution)/shard_map/ppermute | solution.py:590
  47.4 11.0 %collective-permute-start.19 = (bf16[64,2176]{1,0:T(8,128)(2,1)S(1)}, bf16[64,2176]{1,0:T(8,128)(2,1)S(1)}, u32[]{:S(2)}, u32[]{:S(2)}) collective-permute-start(bf16[64,2176]{1,0:T(8,128)(2,1)S(1)} %shard_map.128), channel_id=1, source_target_pairs={{0,2},{1,0},{2,3},{3,1},{4,6},{5,4},{6,7},{7,5},{8,10},{9,8},{10,1... | collective-permute-start | bytes 835592 | tf_op jit(solution)/shard_map/ppermute | solution.py:590
  52.7 12.7 %collective-permute-start.21 = (bf16[64,2176]{1,0:T(8,128)(2,1)S(1)}, bf16[64,2176]{1,0:T(8,128)(2,1)S(1)}, u32[]{:S(2)}, u32[]{:S(2)}) collective-permute-start(bf16[64,2176]{1,0:T(8,128)(2,1)S(1)} %relay.1), channel_id=1, source_target_pairs={{0,1},{1,3},{2,0},{3,2},{4,5},{5,7},{6,4},{7,6},{8,9},{9,11},{10,8... | collective-permute-start | bytes 835592 | tf_op jit(solution)/shard_map/ppermute | solution.py:590

commit v3 on v2

--- a/solution.py
+++ b/solution.py
@@ -156,7 +156,7 @@
 
 def base_kernel(gain_ref, hidden, q_held, kv_held, x_ref, q_out, kv_out):
     rows, wide = hidden.shape
-    depth = 512
+    depth = wide
 
     q_out[...] = jnp.zeros_like(q_out)
     kv_out[...] = jnp.zeros_like(kv_out)
@@ -300,7 +300,7 @@
     scale = 1.0 / math.sqrt(dim)
     count = rows // block
     wide = out_ref.shape[1] - pm_ref.shape[1]
-    size = 512 if wide % 512 == 0 else wide
+    size = wide
     column = chunk_target(far) * wide
 
     total = parts_refs[0][...].astype(F32)
@@ -452,7 +452,7 @@
 
 def chunk_kernel(ctx_ref, w_ref, pm_ref, out_ref, *, k):
     wide = out_ref.shape[1] - (pm_ref.shape[1] if k else 0)
-    size = 512 if wide % 512 == 0 else wide
+    size = wide
     column = chunk_target(k) * wide
 
     def project(n, _):

time: 66.6 us -> 65.7 us (0.986)
  Pallas kernels: 19.1 us -> 15.4 us
  starting transfers between devices: 25.8 us -> 27.3 us
  waiting for transfers between devices: 18.2 us -> 19.5 us
    ppermute x17, starting transfers between devices: 16.5 us -> 18.8 us  [hop(): return lax.ppermute(x, axis, [(i, to(i, k)) for i in range(n)])]
    pallas_call x1, Pallas kernels: 6.8 us -> 4.8 us  [base_projections(): pl.pallas_call(base_kernel, in_specs=[vmem] * 4, out_specs=[vmem] * 3, ou...]
    ppermute x4, waiting for transfers between devices: 10.7 us -> 12.4 us  [sent(): return lax.ppermute(x, 'tp', pairs)]
    pallas_call x3, Pallas kernels: 3.65 us -> 2.52 us  [chunk(): pl.pallas_call(functools.partial(chunk_kernel, k=k), in_specs=[vmem, vmem...]
    ppermute x4, starting transfers between devices: 8.55 us -> 7.77 us  [sent(): return lax.ppermute(x, 'tp', pairs)]
  transfers between devices with their start and end apart: 22 -> 22, of which waited for: 8 -> 8; matrix products, arithmetic and copies ran while one was open for 0% -> 0% of each run, Pallas kernels for 18% -> 14%
where the time goes in v3:
time: 65.7 us; the launch traced here: 65.5 us
  starting transfers between devices  27.3 us (42%)
  waiting for transfers between devices  19.5 us (30%)
  Pallas kernels  15.4 us (23%)
  local copies, waits for them, and re-layouts  3.11 us (5%)
    ppermute x17, starting transfers between devices, hop(): return lax.ppermute(x, axis, [(i, to(i, k)) for i in range(n)])  18.8 us
    ppermute x4, waiting for transfers between devices, sent(): return lax.ppermute(x, 'tp', pairs)  12.4 us
    ppermute x4, starting transfers between devices, sent(): return lax.ppermute(x, 'tp', pairs)  7.77 us
    ppermute x17, waiting for transfers between devices, hop(): return lax.ppermute(x, axis, [(i, to(i, k)) for i in range(n)])  7.12 us
    pallas_call x1, Pallas kernels, attention(): pl.pallas_call(functools.partial(attend_kernel, parts=len(parts), group=h...  5.27 us
    pallas_call x1, Pallas kernels, base_projections(): pl.pallas_call(base_kernel, in_specs=[vmem] * 4, out_specs=[vmem] * 3, ou...  4.8 us
    unnamed x32, local copies, waits for them, and re-layouts  3.11 us
    pallas_call x3, Pallas kernels, chunk(): pl.pallas_call(functools.partial(chunk_kernel, k=k), in_specs=[vmem, vmem...  2.52 us
  transfers between devices with their start and end apart: 22, of which 8 were waited for; matrix products, arithmetic and copies ran while one was open for 0% of the time, Pallas kernels for 14%

profile of v3, /device:TPU:0, one launch (start us, length us, event | category | flops | bytes accessed | tf_op | source)
XLA Modules:
  0.0 65.5 jit_solution(15063852815085097372)
XLA Ops:
  0.0 0.0 copy-start.8
  0.0 0.0 copy-start.7
  0.0 0.0 copy-start.11
  0.1 0.8 %copy-done.10 = bf16[3,256,64]{1,2,0:T(8,128)(2,1)S(1)} copy-done((bf16[3,256,64]{1,2,0:T(8,128)(2,1)S(1)}, bf16[3,256,64]{1,2,0:T(8,128)(2,1)}, u32[]{:S(2)}) %copy-start.10) | copy-done | bytes 98328
  0.9 0.5 collective-permute-start.11
  1.4 3.4 %collective-permute-start.10 = (bf16[192,256]{1,0:T(8,128)(2,1)S(1)}, bf16[192,256]{1,0:T(8,128)(2,1)S(1)}, u32[]{:S(2)}, u32[]{:S(2)}) collective-permute-start(bf16[192,256]{1,0:T(8,128)(2,1)S(1)} %bitcast.11), channel_id=1, source_target_pairs={{0,24},{4,28},{8,16},{12,20},{16,8},{20,12},{24,0},{28,4},{1,25},{... | collective-permute-start | bytes 294920 | tf_op jit(solution)/shard_map/ppermute | solution.py:45
  4.8 0.5 collective-permute-start.9
  5.3 0.1 collective-permute-start.8
  5.4 0.0 copy-done.4
  5.4 0.1 pack.1
  5.5 0.8 %collective-permute-start = (bf16[64,576]{1,0:T(8,128)(2,1)S(1)}, bf16[64,576]{1,0:T(8,128)(2,1)S(1)}, u32[]{:S(2)}, u32[]{:S(2)}) collective-permute-start(bf16[64,576]{1,0:T(8,128)(2,1)S(1)} %pack.1), channel_id=1, source_target_pairs={{0,0},{1,4},{2,8},{3,12},{4,16},{5,20},{6,24},{7,28},{8,1},{9,5},{... | collective-permute-start | bytes 221192 | tf_op jit(solution)/shard_map/ppermute | solution.py:566
  6.3 2.0 %copy-done.7 = bf16[8192,1024]{1,0:T(8,128)(2,1)S(1)} copy-done((bf16[8192,1024]{1,0:T(8,128)(2,1)S(1)}, bf16[8192,1024]{1,0:T(8,128)(2,1)}, u32[]{:S(2)}) %copy-start.7) | copy-done | bytes 16777240
  8.3 0.2 copy-done.9
  8.5 4.8 %base.1 = (bf16[64,8192]{1,0:T(8,128)(2,1)S(1)}, f32[64,1024]{1,0:T(8,128)S(1)}, f32[2,64,256]{2,1,0:T(8,128)S(1)}) custom-call(bf16[64,128]{1,0:T(8,128)(2,1)S(1)} %bitcast.15, bf16[64,8192]{1,0:T(8,128)(2,1)S(1)} %copy-done.9, bf16[8192,1024]{1,0:T(8,128)(2,1)S(1)} %copy-done.7, bf16[2,8192,256]{2,1,0:T(8,128)(2,1)S(1)} %copy-done.8), custom_call_target="tpu_custom_call" | custom-call | flops 12884901888 | bytes 25165824 | tf_op jit(solution)/shard_map/base/pallas_call | solution.py:191
  13.3 0.0 collective-permute-done.refs_0_
  13.3 6.2 %collective-permute-start.3 = (bf16[64,576]{1,0:T(8,128)(2,1)S(1)}, bf16[64,576]{1,0:T(8,128)(2,1)S(1)}, u32[]{:S(2)}, u32[]{:S(2)}) collective-permute-start(bf16[64,576]{1,0:T(8,128)(2,1)S(1)} %collective-permute-done.refs_0_), channel_id=1, source_target_pairs={{0,24},{4,28},{8,16},{12,20},{16,8},{20,12},{24,0},{28,4},{1,25},{... | collective-permute-start | bytes 221192 | tf_op jit(solution)/shard_map/ppermute | solution.py:45
  19.5 0.0 collective-permute-done.10.refs_3_
  19.5 0.0 collective-permute-start.14
  19.5 0.0 collective-permute-done.9.refs_2_
  19.5 0.5 collective-permute-start.13
  20.0 0.0 collective-permute-done.8.refs_1_
  20.0 0.1 collective-permute-start.12
  20.1 0.0 collective-permute-done.11.refs_4_
  20.1 0.3 collective-permute-start.2
  20.4 1.5 %collective-permute-done.3.refs_3_ = bf16[64,576]{1,0:T(8,128)(2,1)S(1)} collective-permute-done((bf16[64,576]{1,0:T(8,128)(2,1)S(1)}, bf16[64,576]{1,0:T(8,128)(2,1)S(1)}, u32[]{:S(2)}, u32[]{:S(2)}) %collective-permute-start.3) | collective-permute-done | bytes 73760 | tf_op jit(solution)/shard_map/ppermute | solution.py:45
  21.9 1.9 %collective-permute-start.1 = (bf16[64,576]{1,0:T(8,128)(2,1)S(1)}, bf16[64,576]{1,0:T(8,128)(2,1)S(1)}, u32[]{:S(2)}, u32[]{:S(2)}) collective-permute-start(bf16[64,576]{1,0:T(8,128)(2,1)S(1)} %collective-permute-done.refs_0_), channel_id=1, source_target_pairs={{0,8},{4,12},{8,0},{12,4},{16,24},{20,28},{24,16},{28,20},{1,9},{5... | collective-permute-start | bytes 221192 | tf_op jit(solution)/shard_map/ppermute | solution.py:45
  23.8 1.1 %collective-permute-done.2.refs_2_ = bf16[64,576]{1,0:T(8,128)(2,1)S(1)} collective-permute-done((bf16[64,576]{1,0:T(8,128)(2,1)S(1)}, bf16[64,576]{1,0:T(8,128)(2,1)S(1)}, u32[]{:S(2)}, u32[]{:S(2)}) %collective-permute-start.2) | collective-permute-done | bytes 73760 | tf_op jit(solution)/shard_map/ppermute | solution.py:45
  24.9 0.0 collective-permute-start.4
  24.9 1.5 %collective-permute-done.1.refs_1_ = bf16[64,576]{1,0:T(8,128)(2,1)S(1)} collective-permute-done((bf16[64,576]{1,0:T(8,128)(2,1)S(1)}, bf16[64,576]{1,0:T(8,128)(2,1)S(1)}, u32[]{:S(2)}, u32[]{:S(2)}) %collective-permute-start.1) | collective-permute-done | bytes 73760 | tf_op jit(solution)/shard_map/ppermute | solution.py:45
  26.4 0.0 collective-permute-start.7
  26.4 0.0 collective-permute-done.14.refs_7_
  26.4 0.5 collective-permute-start.6
  26.9 0.0 collective-permute-done.13.refs_6_
  26.9 0.1 collective-permute-start.5
  27.0 0.0 collective-permute-done.12.refs_5_
  27.0 0.0 copy-start.1
  27.0 0.4 inner.1.refs_0_
  27.4 4.1 %collective-permute-start.17 = (bf16[64,256]{1,0:T(8,128)(2,1)S(1)}, bf16[64,256]{1,0:T(8,128)(2,1)S(1)}, u32[]{:S(2)}, u32[]{:S(2)}) collective-permute-start(bf16[64,256]{1,0:T(8,128)(2,1)S(1)} %inner.1.refs_0_), channel_id=1, source_target_pairs={{0,3},{1,2},{2,1},{3,0},{4,7},{5,6},{6,5},{7,4},{8,11},{9,10},{10,... | collective-permute-start | bytes 98312 | tf_op jit(solution)/shard_map/ppermute | solution.py:45
  31.5 0.0 collective-permute-done.4.refs_4_
  31.5 0.0 collective-permute-start.16
  31.5 0.0 collective-permute-done.7.refs_7_
  31.5 0.6 collective-permute-start.15
  32.1 0.8 %tables.1 = (f32[64,128]{1,0:T(8,128)S(1)}, f32[64,128]{1,0:T(8,128)S(1)}) custom-call(s32[64]{0:T(128)S(1)} %copy-done.6, f32[8,128]{1,0:T(8,128)S(1)} %opening.1._), custom_call_target="tpu_custom_call" | custom-call | tf_op jit(solution)/shard_map/tables/pallas_call | solution.py:146
  32.9 0.0 collective-permute-done.6.refs_6_
  32.9 0.0 collective-permute-done.5.refs_5_
  32.9 0.3 assemble.1
  33.2 0.5 collective-permute-done.17.refs_3_
  33.7 2.6 %collective-permute-done.16.refs_2_ = bf16[64,256]{1,0:T(8,128)(2,1)S(1)} collective-permute-done((bf16[64,256]{1,0:T(8,128)(2,1)S(1)}, bf16[64,256]{1,0:T(8,128)(2,1)S(1)}, u32[]{:S(2)}, u32[]{:S(2)}) %collective-permute-start.16) | collective-permute-done | bytes 32800 | tf_op jit(solution)/shard_map/ppermute | solution.py:45
  36.3 0.0 collective-permute-done.15.refs_1_
  36.3 0.0 slice-done.1
  36.3 5.3 %attend.1 = (bf16[64,1024]{1,0:T(8,128)(2,1)S(1)}, bf16[64,128]{1,0:T(8,128)(2,1)S(1)}, bf16[64,2176]{1,0:T(8,128)(2,1)S(1)}) custom-call(s32[64]{0:T(128)S(1)} %copy-done.6, f32[64,1024]{1,0:T(8,128)S(1)} %get-tuple-element.23.q_ref, f32[2,64,256]{2,1,0:T(8,128)S(1)} %get-tuple-element.24.kv_ref, bf16[64,1024]{1,0:T(8,128)(2,1)S(1)} %get-tuple-element.26.q_up, ...), custom_call_target="tpu_custom_call" | custom-call | flops 536870912 | bytes 8388608 | tf_op jit(solution)/shard_map/attend/pallas_call | solution.py:426
  41.6 2.2 %collective-permute-start.20 = (bf16[64,2176]{1,0:T(8,128)(2,1)S(1)}, bf16[64,2176]{1,0:T(8,128)(2,1)S(1)}, u32[]{:S(2)}, u32[]{:S(2)}) collective-permute-start(bf16[64,2176]{1,0:T(8,128)(2,1)S(1)} %get-tuple-element.38), channel_id=1, source_target_pairs={{0,1},{3,2},{4,5},{7,6},{8,9},{11,10},{12,13},{15,14},{16,17},{19,... | collective-permute-start | bytes 835592 | tf_op jit(solution)/shard_map/ppermute | solution.py:590
  43.9 0.7 %collective-permute-start.18 = (bf16[64,2176]{1,0:T(8,128)(2,1)S(1)}, bf16[64,2176]{1,0:T(8,128)(2,1)S(1)}, u32[]{:S(2)}, u32[]{:S(2)}) collective-permute-start(bf16[64,2176]{1,0:T(8,128)(2,1)S(1)} %get-tuple-element.38), channel_id=1, source_target_pairs={{1,2},{2,1},{5,6},{6,5},{9,10},{10,9},{13,14},{14,13},{17,18},{18,... | collective-permute-start | bytes 835592 | tf_op jit(solution)/shard_map/ppermute | solution.py:590
  44.5 0.8 %shard_map.128 = bf16[64,2176]{1,0:T(8,128)(2,1)S(1)} custom-call(bf16[64,1024]{1,0:T(8,128)(2,1)S(1)} %get-tuple-element.35.ctx_ref, bf16[1024,8192]{1,0:T(8,128)(2,1)S(1)} %bitcast.7, bf16[64,128]{1,0:T(8,128)(2,1)S(1)} %get-tuple-element.36.pm_ref), custom_call_target="tpu_custom_call" | custom-call | flops 268435456 | bytes 4194304 | tf_op jit(solution)/shard_map/pallas_call | solution.py:475
  45.4 2.4 %collective-permute-start.19 = (bf16[64,2176]{1,0:T(8,128)(2,1)S(1)}, bf16[64,2176]{1,0:T(8,128)(2,1)S(1)}, u32[]{:S(2)}, u32[]{:S(2)}) collective-permute-start(bf16[64,2176]{1,0:T(8,128)(2,1)S(1)} %shard_map.128), channel_id=1, source_target_pairs={{0,2},{1,0},{2,3},{3,1},{4,6},{5,4},{6,7},{7,5},{8,10},{9,8},{10,1... | collective-permute-start | bytes 835592 | tf_op jit(solution)/shard_map/ppermute | solution.py:590
  47.8 0.8 %shard_map.129.a_ref = bf16[64,2176]{1,0:T(8,128)(2,1)S(1)} custom-call(bf16[64,1024]{1,0:T(8,128)(2,1)S(1)} %get-tuple-element.35.ctx_ref, bf16[1024,8192]{1,0:T(8,128)(2,1)S(1)} %bitcast.7, bf16[64,128]{1,0:T(8,128)(2,1)S(1)} %get-tuple-element.36.pm_ref), custom_call_target="tpu_custom_call" | custom-call | flops 268435456 | bytes 4194304 | tf_op jit(solution)/shard_map/pallas_call | solution.py:475
  48.6 2.3 %collective-permute-done.20.b_ref = bf16[64,2176]{1,0:T(8,128)(2,1)S(1)} collective-permute-done((bf16[64,2176]{1,0:T(8,128)(2,1)S(1)}, bf16[64,2176]{1,0:T(8,128)(2,1)S(1)}, u32[]{:S(2)}, u32[]{:S(2)}) %collective-permute-start.20) | collective-permute-done | bytes 278560 | tf_op jit(solution)/shard_map/ppermute | solution.py:590
  50.9 0.2 relay.1
  51.1 2.5 %collective-permute-start.21 = (bf16[64,2176]{1,0:T(8,128)(2,1)S(1)}, bf16[64,2176]{1,0:T(8,128)(2,1)S(1)}, u32[]{:S(2)}, u32[]{:S(2)}) collective-permute-start(bf16[64,2176]{1,0:T(8,128)(2,1)S(1)} %relay.1), channel_id=1, source_target_pairs={{0,1},{1,3},{2,0},{3,2},{4,5},{5,7},{6,4},{7,6},{8,9},{9,11},{10,8... | collective-permute-start | bytes 835592 | tf_op jit(solution)/shard_map/ppermute | solution.py:590
  53.6 0.8 %shard_map.127.own_ref = f32[64,2048]{1,0:T(8,128)S(1)} custom-call(bf16[64,1024]{1,0:T(8,128)(2,1)S(1)} %get-tuple-element.35.ctx_ref, bf16[1024,8192]{1,0:T(8,128)(2,1)S(1)} %bitcast.7, bf16[64,128]{1,0:T(8,128)(2,1)S(1)} %get-tuple-element.36.pm_ref), custom_call_target="tpu_custom_call" | custom-call | flops 268435456 | bytes 4194304 | tf_op jit(solution)/shard_map/pallas_call | solution.py:475
  54.4 2.4 %collective-permute-done.19.refs_1_ = bf16[64,2176]{1,0:T(8,128)(2,1)S(1)} collective-permute-done((bf16[64,2176]{1,0:T(8,128)(2,1)S(1)}, bf16[64,2176]{1,0:T(8,128)(2,1)S(1)}, u32[]{:S(2)}, u32[]{:S(2)}) %collective-permute-start.19) | collective-permute-done | bytes 278560 | tf_op jit(solution)/shard_map/ppermute | solution.py:590
  56.9 0.0 collective-permute-done.18.refs_0_
  56.9 7.7 %collective-permute-done.21.refs_2_ = bf16[64,2176]{1,0:T(8,128)(2,1)S(1)} collective-permute-done((bf16[64,2176]{1,0:T(8,128)(2,1)S(1)}, bf16[64,2176]{1,0:T(8,128)(2,1)S(1)}, u32[]{:S(2)}, u32[]{:S(2)}) %collective-permute-start.21) | collective-permute-done | bytes 278560 | tf_op jit(solution)/shard_map/ppermute | solution.py:590
  64.5 1.0 %final.1 = bf16[64,2048]{1,0:T(8,128)(2,1)} custom-call(f32[64,2048]{1,0:T(8,128)S(1)} %shard_map.127.own_ref, bf16[64,128]{1,0:T(8,128)(2,1)S(1)} %get-tuple-element.36.pm_ref, bf16[64,2048]{1,0:T(8,128)(2,1)S(1)} %get-tuple-element.37.up_ref, bf16[64,2176]{1,0:T(8,128)(2,1)S(1)} %collective-permute-done.18.refs_0_, ...), custom_call_target="tpu_custom_call" | custom-call | tf_op jit(solution)/shard_map/final/pallas_call | solution.py:528
  (25 shorter events, 0.0 us)
Async XLA Ops:
  0.0 0.9 %copy-start.10 = (bf16[3,256,64]{1,2,0:T(8,128)(2,1)S(1)}, bf16[3,256,64]{1,2,0:T(8,128)(2,1)}, u32[]{:S(2)}) copy-start(bf16[3,256,64]{1,2,0:T(8,128)(2,1)} %param.18) | copy-start | bytes 294916
  0.0 5.4 %copy-start.2 = (bf16[64,256]{1,0:T(8,128)(2,1)S(1)}, bf16[64,256]{1,0:T(8,128)(2,1)}, u32[]{:S(2)}) copy-start(bf16[64,256]{1,0:T(8,128)(2,1)} %ou_ref.1) | copy-start | bytes 98308
  0.0 5.4 %copy-start.4 = (bf16[128,64]{0,1:T(8,128)(2,1)S(1)}, bf16[128,64]{0,1:T(8,128)(2,1)}, u32[]{:S(2)}) copy-start(bf16[128,64]{0,1:T(8,128)(2,1)} %param.21) | copy-start | bytes 49156
  0.0 5.4 %copy-start.5 = (bf16[2,64,32]{1,2,0:T(8,128)(2,1)S(1)}, bf16[2,64,32]{1,2,0:T(8,128)(2,1)}, u32[]{:S(2)}) copy-start(bf16[2,64,32]{1,2,0:T(8,128)(2,1)} %param.20) | copy-start | bytes 24580
  0.0 5.4 %copy-start.3 = (bf16[64,128]{1,0:T(8,128)(2,1)S(1)}, bf16[64,128]{1,0:T(8,128)(2,1)}, u32[]{:S(2)}) copy-start(bf16[64,128]{1,0:T(8,128)(2,1)} %q_ref.1) | copy-start | bytes 49156
  0.0 6.3 %copy-start.8 = (bf16[2,8192,256]{2,1,0:T(8,128)(2,1)S(1)}, bf16[2,8192,256]{2,1,0:T(8,128)(2,1)}, u32[]{:S(2)}) copy-start(bf16[2,8192,256]{2,1,0:T(8,128)(2,1)} %kv_held.1) | copy-start | bytes 25165828
  0.0 8.3 %copy-start.7 = (bf16[8192,1024]{1,0:T(8,128)(2,1)S(1)}, bf16[8192,1024]{1,0:T(8,128)(2,1)}, u32[]{:S(2)}) copy-start(bf16[8192,1024]{1,0:T(8,128)(2,1)} %q_held.1) | copy-start | bytes 50331652
  0.0 8.3 %copy-start.11 = (bf16[8192]{0:T(1024)(128)(2,1)S(1)}, bf16[8192]{0:T(1024)(128)(2,1)}, u32[]{:S(2)}) copy-start(bf16[8192]{0:T(1024)(128)(2,1)} %param.14) | copy-start | bytes 49156
  0.0 8.5 %copy-start.9 = (bf16[64,8192]{1,0:T(8,128)(2,1)S(1)}, bf16[64,8192]{1,0:T(8,128)(2,1)}, u32[]{:S(2)}) copy-start(bf16[64,8192]{1,0:T(8,128)(2,1)} %hidden.1) | copy-start | bytes 3145732
  0.9 19.2 %collective-permute-start.11 = (bf16[192,256]{1,0:T(8,128)(2,1)S(1)}, bf16[192,256]{1,0:T(8,128)(2,1)S(1)}, u32[]{:S(2)}, u32[]{:S(2)}) collective-permute-start(bf16[192,256]{1,0:T(8,128)(2,1)S(1)} %bitcast.10), channel_id=1, source_target_pairs={{0,4},{4,0},{8,12},{12,8},{16,20},{20,16},{24,28},{28,24},{1,5},{5... | collective-permute-start | bytes 294920 | tf_op jit(solution)/shard_map/ppermute | solution.py:45
  1.4 18.1 %collective-permute-start.10 = (bf16[192,256]{1,0:T(8,128)(2,1)S(1)}, bf16[192,256]{1,0:T(8,128)(2,1)S(1)}, u32[]{:S(2)}, u32[]{:S(2)}) collective-permute-start(bf16[192,256]{1,0:T(8,128)(2,1)S(1)} %bitcast.11), channel_id=1, source_target_pairs={{0,24},{4,28},{8,16},{12,20},{16,8},{20,12},{24,0},{28,4},{1,25},{... | collective-permute-start | bytes 294920 | tf_op jit(solution)/shard_map/ppermute | solution.py:45
  4.8 14.7 %collective-permute-start.9 = (bf16[192,256]{1,0:T(8,128)(2,1)S(1)}, bf16[192,256]{1,0:T(8,128)(2,1)S(1)}, u32[]{:S(2)}, u32[]{:S(2)}) collective-permute-start(bf16[192,256]{1,0:T(8,128)(2,1)S(1)} %bitcast.12), channel_id=1, source_target_pairs={{0,16},{4,20},{8,24},{12,28},{16,0},{20,4},{24,8},{28,12},{1,17},{... | collective-permute-start | bytes 294920 | tf_op jit(solution)/shard_map/ppermute | solution.py:45
  5.3 14.7 %collective-permute-start.8 = (bf16[192,256]{1,0:T(8,128)(2,1)S(1)}, bf16[192,256]{1,0:T(8,128)(2,1)S(1)}, u32[]{:S(2)}, u32[]{:S(2)}) collective-permute-start(bf16[192,256]{1,0:T(8,128)(2,1)S(1)} %bitcast.13), channel_id=1, source_target_pairs={{0,8},{4,12},{8,0},{12,4},{16,24},{20,28},{24,16},{28,20},{1,9},{5... | collective-permute-start | bytes 294920 | tf_op jit(solution)/shard_map/ppermute | solution.py:45
  5.5 7.8 %collective-permute-start = (bf16[64,576]{1,0:T(8,128)(2,1)S(1)}, bf16[64,576]{1,0:T(8,128)(2,1)S(1)}, u32[]{:S(2)}, u32[]{:S(2)}) collective-permute-start(bf16[64,576]{1,0:T(8,128)(2,1)S(1)} %pack.1), channel_id=1, source_target_pairs={{0,0},{1,4},{2,8},{3,12},{4,16},{5,20},{6,24},{7,28},{8,1},{9,5},{... | collective-permute-start | bytes 221192 | tf_op jit(solution)/shard_map/ppermute | solution.py:566
  8.5 27.8 %slice-start = ((s8[16777216]{0:T(1024)(128)(4,1)}), s8[4194304]{0:T(1024)(128)(4,1)S(1)}, s32[]{:S(2)}) async-start(s8[16777216]{0:T(1024)(128)(4,1)} %bitcast.6), calls=%async_computation | async-start | bytes 8388608
  8.5 27.8 %slice-start.1 = ((s8[16777216]{0:T(1024)(128)(4,1)}), s8[4194304]{0:T(1024)(128)(4,1)S(1)}, s32[]{:S(2)}) async-start(s8[16777216]{0:T(1024)(128)(4,1)} %bitcast.6), calls=%async_computation.1 | async-start | bytes 8388608
  8.5 27.8 %slice-start.2 = ((s8[16777216]{0:T(1024)(128)(4,1)}), s8[4194304]{0:T(1024)(128)(4,1)S(1)}, s32[]{:S(2)}) async-start(s8[16777216]{0:T(1024)(128)(4,1)} %bitcast.6), calls=%async_computation.2 | async-start | bytes 8388608
  13.3 8.6 %collective-permute-start.3 = (bf16[64,576]{1,0:T(8,128)(2,1)S(1)}, bf16[64,576]{1,0:T(8,128)(2,1)S(1)}, u32[]{:S(2)}, u32[]{:S(2)}) collective-permute-start(bf16[64,576]{1,0:T(8,128)(2,1)S(1)} %collective-permute-done.refs_0_), channel_id=1, source_target_pairs={{0,24},{4,28},{8,16},{12,20},{16,8},{20,12},{24,0},{28,4},{1,25},{... | collective-permute-start | bytes 221192 | tf_op jit(solution)/shard_map/ppermute | solution.py:45
  19.5 6.9 %collective-permute-start.14 = (bf16[192,256]{1,0:T(8,128)(2,1)S(1)}, bf16[192,256]{1,0:T(8,128)(2,1)S(1)}, u32[]{:S(2)}, u32[]{:S(2)}) collective-permute-start(bf16[192,256]{1,0:T(8,128)(2,1)S(1)} %collective-permute-done.10.refs_3_), channel_id=1, source_target_pairs={{0,4},{4,0},{8,12},{12,8},{16,20},{20,16},{24,28},{28,24},{1,5},{5... | collective-permute-start | bytes 294920 | tf_op jit(solution)/shard_map/ppermute | solution.py:45
  19.5 7.4 %collective-permute-start.13 = (bf16[192,256]{1,0:T(8,128)(2,1)S(1)}, bf16[192,256]{1,0:T(8,128)(2,1)S(1)}, u32[]{:S(2)}, u32[]{:S(2)}) collective-permute-start(bf16[192,256]{1,0:T(8,128)(2,1)S(1)} %collective-permute-done.9.refs_2_), channel_id=1, source_target_pairs={{0,4},{4,0},{8,12},{12,8},{16,20},{20,16},{24,28},{28,24},{1,5},{5... | collective-permute-start | bytes 294920 | tf_op jit(solution)/shard_map/ppermute | solution.py:45
  20.0 6.9 %collective-permute-start.12 = (bf16[192,256]{1,0:T(8,128)(2,1)S(1)}, bf16[192,256]{1,0:T(8,128)(2,1)S(1)}, u32[]{:S(2)}, u32[]{:S(2)}) collective-permute-start(bf16[192,256]{1,0:T(8,128)(2,1)S(1)} %collective-permute-done.8.refs_1_), channel_id=1, source_target_pairs={{0,4},{4,0},{8,12},{12,8},{16,20},{20,16},{24,28},{28,24},{1,5},{5... | collective-permute-start | bytes 294920 | tf_op jit(solution)/shard_map/ppermute | solution.py:45
  20.1 4.8 %collective-permute-start.2 = (bf16[64,576]{1,0:T(8,128)(2,1)S(1)}, bf16[64,576]{1,0:T(8,128)(2,1)S(1)}, u32[]{:S(2)}, u32[]{:S(2)}) collective-permute-start(bf16[64,576]{1,0:T(8,128)(2,1)S(1)} %collective-permute-done.refs_0_), channel_id=1, source_target_pairs={{0,16},{4,20},{8,24},{12,28},{16,0},{20,4},{24,8},{28,12},{1,17},{... | collective-permute-start | bytes 221192 | tf_op jit(solution)/shard_map/ppermute | solution.py:45
  21.9 4.4 %collective-permute-start.1 = (bf16[64,576]{1,0:T(8,128)(2,1)S(1)}, bf16[64,576]{1,0:T(8,128)(2,1)S(1)}, u32[]{:S(2)}, u32[]{:S(2)}) collective-permute-start(bf16[64,576]{1,0:T(8,128)(2,1)S(1)} %collective-permute-done.refs_0_), channel_id=1, source_target_pairs={{0,8},{4,12},{8,0},{12,4},{16,24},{20,28},{24,16},{28,20},{1,9},{5... | collective-permute-start | bytes 221192 | tf_op jit(solution)/shard_map/ppermute | solution.py:45
  24.9 6.6 %collective-permute-start.4 = (bf16[64,576]{1,0:T(8,128)(2,1)S(1)}, bf16[64,576]{1,0:T(8,128)(2,1)S(1)}, u32[]{:S(2)}, u32[]{:S(2)}) collective-permute-start(bf16[64,576]{1,0:T(8,128)(2,1)S(1)} %collective-permute-done.refs_0_), channel_id=1, source_target_pairs={{0,4},{4,0},{8,12},{12,8},{16,20},{20,16},{24,28},{28,24},{1,5},{5... | collective-permute-start | bytes 221192 | tf_op jit(solution)/shard_map/ppermute | solution.py:45
  26.4 5.1 %collective-permute-start.7 = (bf16[64,576]{1,0:T(8,128)(2,1)S(1)}, bf16[64,576]{1,0:T(8,128)(2,1)S(1)}, u32[]{:S(2)}, u32[]{:S(2)}) collective-permute-start(bf16[64,576]{1,0:T(8,128)(2,1)S(1)} %collective-permute-done.3.refs_3_), channel_id=1, source_target_pairs={{0,4},{4,0},{8,12},{12,8},{16,20},{20,16},{24,28},{28,24},{1,5},{5... | collective-permute-start | bytes 221192 | tf_op jit(solution)/shard_map/ppermute | solution.py:45
  26.4 6.5 %collective-permute-start.6 = (bf16[64,576]{1,0:T(8,128)(2,1)S(1)}, bf16[64,576]{1,0:T(8,128)(2,1)S(1)}, u32[]{:S(2)}, u32[]{:S(2)}) collective-permute-start(bf16[64,576]{1,0:T(8,128)(2,1)S(1)} %collective-permute-done.2.refs_2_), channel_id=1, source_target_pairs={{0,4},{4,0},{8,12},{12,8},{16,20},{20,16},{24,28},{28,24},{1,5},{5... | collective-permute-start | bytes 221192 | tf_op jit(solution)/shard_map/ppermute | solution.py:45
  26.9 6.0 %collective-permute-start.5 = (bf16[64,576]{1,0:T(8,128)(2,1)S(1)}, bf16[64,576]{1,0:T(8,128)(2,1)S(1)}, u32[]{:S(2)}, u32[]{:S(2)}) collective-permute-start(bf16[64,576]{1,0:T(8,128)(2,1)S(1)} %collective-permute-done.1.refs_1_), channel_id=1, source_target_pairs={{0,4},{4,0},{8,12},{12,8},{16,20},{20,16},{24,28},{28,24},{1,5},{5... | collective-permute-start | bytes 221192 | tf_op jit(solution)/shard_map/ppermute | solution.py:45
  27.0 5.1 %copy-start.6 = (s32[64]{0:T(128)S(1)}, s32[64]{0:T(128)}, u32[]{:S(2)}) copy-start(s32[64]{0:T(128)} %lengths_ref.3) | copy-start | bytes 772
  27.0 9.3 %slice-start.3 = ((s8[16777216]{0:T(1024)(128)(4,1)}), s8[4194304]{0:T(1024)(128)(4,1)S(1)}, s32[]{:S(2)}) async-start(s8[16777216]{0:T(1024)(128)(4,1)} %bitcast.6), calls=%async_computation.3 | async-start | bytes 8388608
  27.0 9.3 %copy-start = (bf16[64,2,128,128]{3,2,1,0:T(8,128)(2,1)S(1)}, bf16[64,2,128,128]{3,2,1,0:T(8,128)(2,1)}, u32[]{:S(2)}) copy-start(bf16[64,2,128,128]{3,2,1,0:T(8,128)(2,1)} %refs_4_.1) | copy-start | bytes 12582916
  27.0 9.3 %copy-start.1 = (bf16[64,2,128,128]{3,2,1,0:T(8,128)(2,1)S(1)}, bf16[64,2,128,128]{3,2,1,0:T(8,128)(2,1)}, u32[]{:S(2)}) copy-start(bf16[64,2,128,128]{3,2,1,0:T(8,128)(2,1)} %refs_5_.1) | copy-start | bytes 12582916
  27.4 6.3 %collective-permute-start.17 = (bf16[64,256]{1,0:T(8,128)(2,1)S(1)}, bf16[64,256]{1,0:T(8,128)(2,1)S(1)}, u32[]{:S(2)}, u32[]{:S(2)}) collective-permute-start(bf16[64,256]{1,0:T(8,128)(2,1)S(1)} %inner.1.refs_0_), channel_id=1, source_target_pairs={{0,3},{1,2},{2,1},{3,0},{4,7},{5,6},{6,5},{7,4},{8,11},{9,10},{10,... | collective-permute-start | bytes 98312 | tf_op jit(solution)/shard_map/ppermute | solution.py:45
  31.5 4.8 %collective-permute-start.16 = (bf16[64,256]{1,0:T(8,128)(2,1)S(1)}, bf16[64,256]{1,0:T(8,128)(2,1)S(1)}, u32[]{:S(2)}, u32[]{:S(2)}) collective-permute-start(bf16[64,256]{1,0:T(8,128)(2,1)S(1)} %inner.1.refs_0_), channel_id=1, source_target_pairs={{0,2},{1,3},{2,0},{3,1},{4,6},{5,7},{6,4},{7,5},{8,10},{9,11},{10,... | collective-permute-start | bytes 98312 | tf_op jit(solution)/shard_map/ppermute | solution.py:45
  31.5 4.8 %collective-permute-start.15 = (bf16[64,256]{1,0:T(8,128)(2,1)S(1)}, bf16[64,256]{1,0:T(8,128)(2,1)S(1)}, u32[]{:S(2)}, u32[]{:S(2)}) collective-permute-start(bf16[64,256]{1,0:T(8,128)(2,1)S(1)} %inner.1.refs_0_), channel_id=1, source_target_pairs={{0,1},{1,0},{2,3},{3,2},{4,5},{5,4},{6,7},{7,6},{8,9},{9,8},{10,11... | collective-permute-start | bytes 98312 | tf_op jit(solution)/shard_map/ppermute | solution.py:45
  41.6 9.3 %collective-permute-start.20 = (bf16[64,2176]{1,0:T(8,128)(2,1)S(1)}, bf16[64,2176]{1,0:T(8,128)(2,1)S(1)}, u32[]{:S(2)}, u32[]{:S(2)}) collective-permute-start(bf16[64,2176]{1,0:T(8,128)(2,1)S(1)} %get-tuple-element.38), channel_id=1, source_target_pairs={{0,1},{3,2},{4,5},{7,6},{8,9},{11,10},{12,13},{15,14},{16,17},{19,... | collective-permute-start | bytes 835592 | tf_op jit(solution)/shard_map/ppermute | solution.py:590
  43.9 13.0 %collective-permute-start.18 = (bf16[64,2176]{1,0:T(8,128)(2,1)S(1)}, bf16[64,2176]{1,0:T(8,128)(2,1)S(1)}, u32[]{:S(2)}, u32[]{:S(2)}) collective-permute-start(bf16[64,2176]{1,0:T(8,128)(2,1)S(1)} %get-tuple-element.38), channel_id=1, source_target_pairs={{1,2},{2,1},{5,6},{6,5},{9,10},{10,9},{13,14},{14,13},{17,18},{18,... | collective-permute-start | bytes 835592 | tf_op jit(solution)/shard_map/ppermute | solution.py:590
  45.4 11.5 %collective-permute-start.19 = (bf16[64,2176]{1,0:T(8,128)(2,1)S(1)}, bf16[64,2176]{1,0:T(8,128)(2,1)S(1)}, u32[]{:S(2)}, u32[]{:S(2)}) collective-permute-start(bf16[64,2176]{1,0:T(8,128)(2,1)S(1)} %shard_map.128), channel_id=1, source_target_pairs={{0,2},{1,0},{2,3},{3,1},{4,6},{5,4},{6,7},{7,5},{8,10},{9,8},{10,1... | collective-permute-start | bytes 835592 | tf_op jit(solution)/shard_map/ppermute | solution.py:590
  51.1 13.4 %collective-permute-start.21 = (bf16[64,2176]{1,0:T(8,128)(2,1)S(1)}, bf16[64,2176]{1,0:T(8,128)(2,1)S(1)}, u32[]{:S(2)}, u32[]{:S(2)}) collective-permute-start(bf16[64,2176]{1,0:T(8,128)(2,1)S(1)} %relay.1), channel_id=1, source_target_pairs={{0,1},{1,3},{2,0},{3,2},{4,5},{5,7},{6,4},{7,6},{8,9},{9,11},{10,8... | collective-permute-start | bytes 835592 | tf_op jit(solution)/shard_map/ppermute | solution.py:590
